TPU v7x, 32 devices: a 4x4x1 block of a 4x4x8 slice. The times are simulated.
32 devices in a mesh: dp: 1 (over z), tp: 4 (over y), fsdp: 8 (over x, core).
Axes of the slice: x: 4, y: 4, z: 1, core: 2. Of those that a mesh axis runs over, the one named last changes fastest.
The devices are a block of a 4x4x8 slice.
Arguments:
- x: bfloat16 [32, 1024, 2048], P(('dp', 'fsdp'))
- w_query: bfloat16 [2, 2048, 2048], P(None, 'fsdp', 'tp')
- w_key: bfloat16 [2, 2048, 2048], P(None, 'fsdp', 'tp')
- w_value: bfloat16 [2, 2048, 2048], P(None, 'fsdp', 'tp')
- w_out: bfloat16 [2, 2048, 2048], P(None, 'tp', 'fsdp')
- w_gate: bfloat16 [2, 2048, 8192], P(None, 'fsdp', 'tp')
- w_up: bfloat16 [2, 2048, 8192], P(None, 'fsdp', 'tp')
- w_down: bfloat16 [2, 8192, 2048], P(None, 'tp', 'fsdp')
- q_norm_w: float32 [2, 2048], P(None, 'tp')
- k_norm_w: float32 [2, 2048], P(None, 'tp')
- attn_norm_w: float32 [2, 2048], P(None, 'fsdp')
- ffn_norm_w: float32 [2, 2048], P(None, 'fsdp')
Outputs:
- output 1: bfloat16 [32, 1024, 2048], P(('dp', 'fsdp'))
- output 2: bfloat16 [2, 32, 1024, 16, 128], P(None, ('dp', 'fsdp'), None, 'tp')
- output 3: bfloat16 [2, 32, 1024, 16, 128], P(None, ('dp', 'fsdp'), None, 'tp')
All inputs are finite; a program needn't handle non-finite values.
Results may differ from a plain program's by a relative error of at most 0.02.
Values are sent between devices in bfloat16 or wider.
A program may use at most 768 MiB of HBM per device.

v0:
```python
import jax
import jax.numpy as jnp
from jax import lax
from jax.experimental import pallas as pl
from jax.experimental.pallas import tpu as pltpu
from jax.sharding import PartitionSpec as P


HEAD_DIM = 128
NORM_EPS = 1e-6
ROPE_THETA = 500000.0
CHUNKS = 2
QB = 256
F32, BF16 = jnp.float32, jnp.bfloat16


def rope_tables(seq_len):
    half = HEAD_DIM // 2
    inv_freq = ROPE_THETA ** (-2.0 * jnp.arange(half, dtype=F32) / HEAD_DIM)
    angles = jnp.arange(seq_len, dtype=F32)[:, None] * inv_freq[None, :]
    cos_t, sin_t = jnp.cos(angles), jnp.sin(angles)
    return jnp.concatenate([cos_t, cos_t], axis=-1), jnp.concatenate([-sin_t, sin_t], axis=-1)


def dot(a, b):
    return jnp.dot(a, b, preferred_element_type=F32)


def params(*semantics):
    return pltpu.CompilerParams(dimension_semantics=semantics or ("arbitrary",), vmem_limit_bytes=60 * 1024 * 1024)


def cost(flops, nbytes):
    return pl.CostEstimate(flops=flops, bytes_accessed=nbytes, transcendentals=0)


def rotate(vals, cos_t, sin_t):
    return vals * cos_t + pltpu.roll(vals, HEAD_DIM // 2, 1) * sin_t


def qkv_raw(x, w):
    tokens, width = x.shape
    part = w.shape[1] // 3
    tm = min(512, tokens)

    def body(x_ref, w_ref, q_ref, k_ref, v_ref, sq_ref):
        xb = x_ref[...]
        q = dot(xb, w_ref[:, :part])
        q_ref[...] = q
        q_sq = jnp.sum(q * q, axis=-1, keepdims=True)
        k = dot(xb, w_ref[:, part:2 * part])
        k_ref[...] = k
        k_sq = jnp.sum(k * k, axis=-1, keepdims=True)
        v_ref[...] = dot(xb, w_ref[:, 2 * part:]).astype(BF16)
        lane = lax.broadcasted_iota(jnp.int32, (tm, 128), 1)
        cols = jnp.where(lane == 0, q_sq, jnp.where(lane == 1, k_sq, 0.0))
        sq_ref[...] = cols.T[:8, :]

    row = lambda i: (i, 0)
    return pl.pallas_call(
        body, grid=(tokens // tm,),
        in_specs=[pl.BlockSpec((tm, width), row), pl.BlockSpec(w.shape, lambda i: (0, 0), pipeline_mode=pl.Buffered(1))],
        out_specs=[pl.BlockSpec((tm, part), row)] * 3 + [pl.BlockSpec((8, tm), lambda i: (0, i))],
        out_shape=[jax.ShapeDtypeStruct((tokens, part), d) for d in (F32, F32, BF16)]
        + [jax.ShapeDtypeStruct((8, tokens), F32)],
        compiler_params=params(), cost_estimate=cost(2 * tokens * width * 3 * part, 2 * tokens * width + 10 * tokens * part),
        name="qkv_raw")(x, w)


def norm_rope(q_raw, k_raw, inv, q_gain, k_gain, cos_t, sin_t):
    tokens, part = q_raw.shape
    tm = min(512, cos_t.shape[0])
    per_seq = cos_t.shape[0] // tm

    def body(q_ref, k_ref, inv_ref, qg_ref, kg_ref, cos_ref, sin_ref, qo_ref, ko_ref):
        for n, (src, gain, dst) in enumerate(((q_ref, qg_ref, qo_ref), (k_ref, kg_ref, ko_ref))):
            scale = jnp.broadcast_to(inv_ref[n:n + 1, :], (128, tm)).T
            for h in range(part // HEAD_DIM):
                cols = slice(h * HEAD_DIM, (h + 1) * HEAD_DIM)
                vals = src[:, cols] * scale * gain[:, cols]
                dst[:, cols] = rotate(vals, cos_ref[...], sin_ref[...]).astype(BF16)

    row = lambda i: (i, 0)
    gain = pl.BlockSpec((1, part), lambda i: (0, 0))
    table = pl.BlockSpec((tm, HEAD_DIM), lambda i: (lax.rem(i, per_seq), 0))
    return pl.pallas_call(
        body, grid=(tokens // tm,),
        in_specs=[pl.BlockSpec((tm, part), row)] * 2 + [pl.BlockSpec((8, tm), lambda i: (0, i)), gain, gain, table, table],
        out_specs=[pl.BlockSpec((tm, part), row)] * 2,
        out_shape=[jax.ShapeDtypeStruct((tokens, part), BF16)] * 2,
        compiler_params=params(), cost_estimate=cost(tokens * part * 2000, tokens * part * 12),
        name="norm_rope")(q_raw, k_raw, inv, q_gain, k_gain, cos_t, sin_t)


def softmax_pv(q, past, k, v):
    rows = q.shape[0]
    nt = (((1,), (1,)), ((), ()))
    scale = HEAD_DIM ** -0.5
    diag = lax.dot_general(q, k, nt, preferred_element_type=F32) * scale
    keep = lax.broadcasted_iota(jnp.int32, (rows, rows), 0) >= lax.broadcasted_iota(jnp.int32, (rows, rows), 1)
    diag = jnp.where(keep, diag, -jnp.inf)
    top = jnp.max(diag, axis=-1, keepdims=True)
    scores = [(lax.dot_general(q, pk, nt, preferred_element_type=F32) * scale, pv) for pk, pv in past]
    for left, _ in scores:
        top = jnp.maximum(top, jnp.max(left, axis=-1, keepdims=True))
    probs = [(jnp.exp(left - top), pv) for left, pv in scores] + [(jnp.exp(diag - top), v)]
    total = sum(jnp.sum(p, axis=-1, keepdims=True) for p, _ in probs)
    inv = 1.0 / total
    out = sum(dot((p * inv).astype(BF16), pv) for p, pv in probs)
    return out.astype(BF16)


def attention(q, q_block, qc, kvs):
    seqs, _, group = q.shape
    qb = min(QB, qc)
    heads = group // HEAD_DIM
    half = group // 2
    own = kvs[-1][2] - qc

    def body(q_ref, *refs):
        k_refs, v_refs, (a_ref, b_ref) = refs[:len(kvs)], refs[len(kvs):2 * len(kvs)], refs[2 * len(kvs):]
        for h in range(heads):
            cols = slice(h * HEAD_DIM, (h + 1) * HEAD_DIM)
            dst = (a_ref, b_ref)[h * HEAD_DIM // half]
            dcols = slice(h * HEAD_DIM % half, h * HEAD_DIM % half + HEAD_DIM)
            for j in range(qc // qb):
                first = own + j * qb
                past = [(k_refs[n][0, :, cols], v_refs[n][0, :, cols]) for n in range(len(kvs) - 1)]
                if first:
                    past.append((k_refs[-1][0, :first, cols], v_refs[-1][0, :first, cols]))
                dst[0, j * qb:(j + 1) * qb, dcols] = softmax_pv(
                    q_ref[0, j * qb:(j + 1) * qb, cols], past,
                    k_refs[-1][0, first:first + qb, cols], v_refs[-1][0, first:first + qb, cols])

    kv = [pl.BlockSpec((1, rows, group), lambda s: (s, 0, 0)) for _, _, rows in kvs]
    keys = sum(rows for _, _, rows in kvs)
    out = pl.BlockSpec((1, qc, half), lambda s: (s, 0, 0))
    return pl.pallas_call(
        body, grid=(seqs,),
        in_specs=[pl.BlockSpec((1, qc, group), lambda s: (s, q_block, 0))] + kv + kv,
        out_specs=[out, out],
        out_shape=[jax.ShapeDtypeStruct((seqs, qc, half), BF16)] * 2,
        compiler_params=params(),
        cost_estimate=cost(8 * seqs * qc * keys * group, seqs * group * 2 * (2 * qc + 2 * keys)))(q, *(k for k, _, _ in kvs), *(v for _, v, _ in kvs))


def out_proj_gathered(order, outs, w, x, gain, chunk):
    seqs, qc, half = outs[0].shape
    width = x.shape[2]
    shards, sources, _, cols = w.shape

    def body(order_ref, *refs):
        o_refs, (w_ref, x_ref, gain_ref, ha_ref, hb_ref, a_ref) = refs[:2 * sources], refs[2 * sources:]
        sq = jnp.zeros((qc, 1), F32)
        for f in range(shards):
            acc = jnp.zeros((qc, cols), F32)
            for s in range(sources):
                src = order_ref[s]
                acc += dot(o_refs[2 * s][0], w_ref[f, src, :half, :])
                acc += dot(o_refs[2 * s + 1][0], w_ref[f, src, half:, :])
            a = acc.astype(BF16)
            a_ref[:, f * cols:(f + 1) * cols] = a
            a = a.astype(F32)
            sq += jnp.sum(a * a, axis=-1, keepdims=True)
        inv = lax.rsqrt(sq / width + NORM_EPS)
        for f in range(shards):
            c = slice(f * cols, (f + 1) * cols)
            h_ref = (ha_ref, hb_ref)[f // (shards // 2)]
            hc = slice(f % (shards // 2) * cols, (f % (shards // 2) + 1) * cols)
            h_ref[0, :, hc] = (x_ref[0, :, c].astype(F32) + a_ref[:, c].astype(F32) * inv * gain_ref[:, c]).astype(BF16)

    o_spec = pl.BlockSpec((1, qc, half), lambda r, order: (order[r], 0, 0))
    return pl.pallas_call(
        body,
        grid_spec=pltpu.PrefetchScalarGridSpec(
            num_scalar_prefetch=1, grid=(seqs,),
            in_specs=[o_spec] * (2 * sources) + [
                pl.BlockSpec(w.shape, lambda r, order: (0, 0, 0, 0), pipeline_mode=pl.Buffered(1)),
                pl.BlockSpec((1, qc, width), lambda r, order: (order[r], chunk, 0)),
                pl.BlockSpec((1, width), lambda r, order: (0, 0))],
            out_specs=[pl.BlockSpec((1, qc, width // 2), lambda r, order: (r, 0, 0))] * 2,
            scratch_shapes=[pltpu.VMEM((qc, width), BF16)]),
        out_shape=[jax.ShapeDtypeStruct((seqs, qc, width // 2), BF16)] * 2,
        compiler_params=params(), cost_estimate=cost(2 * seqs * qc * width * width, 6 * seqs * qc * width + 2 * width * width))(order, *outs, w, x, gain)


def mlp_up(hs, w, gate_spec, up_spec, first, steps):
    seqs = len(hs)
    qc, half = hs[0][0].shape
    width = 2 * half
    tn = 256

    def body(*refs):
        h_refs, (g_ref, u_ref, act_ref) = refs[:2 * seqs], refs[2 * seqs:]
        g = g_ref[...].reshape(width, tn)
        u = u_ref[...].reshape(width, tn)
        for s in range(seqs):
            ha, hb = h_refs[2 * s][...], h_refs[2 * s + 1][...]
            gate = dot(ha, g[:half]) + dot(hb, g[half:])
            up = dot(ha, u[:half]) + dot(hb, u[half:])
            act_ref[s * qc:(s + 1) * qc, :] = (jax.nn.silu(gate) * up).astype(BF16)

    index = lambda i: first + i
    fixed = pl.BlockSpec((qc, half), lambda i: (0, 0), pipeline_mode=pl.Buffered(1))
    rows = seqs * qc
    flat = [a for pair in hs for a in pair]
    return pl.pallas_call(
        body, grid=(steps,),
        in_specs=[fixed] * (2 * seqs) + [gate_spec(index), up_spec(index)],
        out_specs=pl.BlockSpec((rows, tn), lambda i: (0, i)),
        out_shape=jax.ShapeDtypeStruct((rows, steps * tn), BF16),
        compiler_params=params(), cost_estimate=cost(4 * rows * width * steps * tn, 2 * rows * width + 4 * width * steps * tn))(*flat, w, w)


def mlp_down(acts, w, down_spec, seqs, width):
    rows = acts[0].shape[0]
    qc = rows // seqs
    ff = sum(a.shape[1] for a in acts)
    n = len(acts)
    tn = 256
    half = width // 2
    per_side = half // tn

    def body(*refs):
        act_refs, d_ref, outs = refs[:n], refs[n], refs[n + 1:]
        d = d_ref[...].reshape(ff, tn)
        step = pl.program_id(0)

        def product(s):
            acc = jnp.zeros((qc, tn), F32)
            at = 0
            for a in act_refs:
                acc += dot(a[s * qc:(s + 1) * qc, :], d[at:at + a.shape[1]])
                at += a.shape[1]
            return acc.astype(BF16)

        for side in range(2):
            @pl.when(step // per_side == side)
            def _(side=side):
                for s in range(seqs):
                    outs[2 * s + side][...] = product(s)

    first = pl.BlockSpec((qc, tn), lambda i: (0, jnp.minimum(i, per_side - 1)))
    second = pl.BlockSpec((qc, tn), lambda i: (0, jnp.maximum(i - per_side, 0)))
    return pl.pallas_call(
        body, grid=(2 * per_side,),
        in_specs=[pl.BlockSpec(a.shape, lambda i: (0, 0), pipeline_mode=pl.Buffered(1)) for a in acts] + [down_spec(lambda i: i)],
        out_specs=[first, second] * seqs,
        out_shape=[jax.ShapeDtypeStruct((qc, half), BF16)] * (2 * seqs),
        compiler_params=params(), cost_estimate=cost(2 * rows * width * ff, 2 * rows * (width + ff) + 2 * width * ff))(*acts, w)


def finish(parts_a, parts_b, h_a, h_b, gain, place, whole):
    rows, half = h_a.shape
    width = 2 * half
    block = 256
    per_side = half // block
    tr = min(256, rows)
    n = len(parts_a)

    def body(*refs):
        pa, pb = refs[:n], refs[n:2 * n]
        h_refs, gain_ref, outs = refs[2 * n:2 * n + 2], refs[2 * n + 2], refs[2 * n + 3:]
        sums = []
        for side in (pa, pb):
            m = side[0][...].astype(F32)
            for p in side[1:]:
                m = m + p[...].astype(F32)
            sums.append(m.astype(BF16).astype(F32))
        sq = sum(jnp.sum(m * m, axis=-1, keepdims=True) for m in sums)
        inv = lax.rsqrt(sq / width + NORM_EPS)
        for side in range(2):
            for b in range(per_side):
                c = slice(b * block, (b + 1) * block)
                at = place(side, b)
                gain_cols = gain_ref[:, at * block:(at + 1) * block]
                val = (h_refs[side][:, c].astype(F32) + sums[side][:, c] * inv * gain_cols).astype(BF16)
                if whole:
                    outs[0][:, at * block:(at + 1) * block] = val
                else:
                    at_half = at % per_side
                    outs[at // per_side][:, at_half * block:(at_half + 1) * block] = val

    part = pl.BlockSpec((tr, half), lambda i: (i, 0))
    out_width = width if whole else half
    outs = 1 if whole else 2
    return pl.pallas_call(
        body, grid=(rows // tr,),
        in_specs=[part] * (2 * n + 2) + [pl.BlockSpec((1, width), lambda i: (0, 0))],
        out_specs=[pl.BlockSpec((tr, out_width), lambda i: (i, 0))] * outs,
        out_shape=[jax.ShapeDtypeStruct((rows, out_width), BF16)] * outs,
        compiler_params=params(), cost_estimate=cost(rows * width * 2000, rows * width * 2 * (n + 2)))(*parts_a, *parts_b, h_a, h_b, gain)


def qkv_full(x, w, q_gain, k_gain, cos_t, sin_t, part, chunk):
    tokens, width = x.shape
    shards, tps, _, cols = w.shape
    depth = width // shards
    per = part // cols
    blocks = tps * per
    tr = min(256, tokens)

    def body(x_ref, w_ref, qg_ref, kg_ref, cos_ref, sin_ref, q_ref, k_ref, v_ref, raw_ref, sq_ref):
        which, n = pl.program_id(0), pl.program_id(1)
        out = dot(x_ref[...], w_ref[...].reshape(width, cols))

        @pl.when(which < 2)
        def _():
            raw_ref[n] = out
            part_sq = jnp.sum(out * out, axis=-1, keepdims=True)
            sq_ref[...] = jnp.where(n == 0, 0.0, sq_ref[...]) + part_sq

        @pl.when(which == 2)
        def _():
            v_ref[0] = out.astype(BF16)

        for sel, (gain, dst) in enumerate(((qg_ref, q_ref), (kg_ref, k_ref))):
            @pl.when((which == sel) & (n == blocks - 1))
            def _(gain=gain, dst=dst):
                def rows_body(r, _):
                    rows = pl.ds(r * tr, tr)
                    inv = lax.rsqrt(sq_ref[rows, :] / width + NORM_EPS)
                    for m in range(blocks):
                        for h in range(cols // HEAD_DIM):
                            lanes = slice(h * HEAD_DIM, (h + 1) * HEAD_DIM)
                            wide = slice(m * cols + h * HEAD_DIM, m * cols + (h + 1) * HEAD_DIM)
                            deep = slice(m % per * cols + h * HEAD_DIM, m % per * cols + (h + 1) * HEAD_DIM)
                            vals = raw_ref[m, rows, lanes] * inv * gain[:, wide]
                            dst[m // per, rows, deep] = rotate(vals, cos_ref[rows, :], sin_ref[rows, :]).astype(BF16)
                    return 0

                lax.fori_loop(0, tokens // tr, rows_body, 0)

    fixed = lambda s: pl.BlockSpec(s, lambda i, n: (0,) * len(s), pipeline_mode=pl.Buffered(1))
    whole = pl.BlockSpec((tps, tokens, part), lambda i, n: (0, 0, 0))
    table = pl.BlockSpec((tokens, HEAD_DIM), lambda i, n: (chunk, 0), pipeline_mode=pl.Buffered(1))
    return pl.pallas_call(
        body, grid=(3, blocks),
        in_specs=[fixed((tokens, width)),
                  pl.BlockSpec((shards, 1, depth, cols), lambda i, n: (0, n // per, i * per + n % per, 0)),
                  fixed((1, width)), fixed((1, width)), table, table],
        out_specs=[whole, whole, pl.BlockSpec((1, tokens, cols), lambda i, n: (jnp.where(i == 2, n // per, 0), 0, jnp.where(i == 2, n % per, 0)))],
        out_shape=[jax.ShapeDtypeStruct((tps, tokens, part), BF16)] * 3,
        scratch_shapes=[pltpu.VMEM((blocks, tokens, cols), F32), pltpu.VMEM((tokens, 1), F32)],
        compiler_params=params("arbitrary", "arbitrary"),
        cost_estimate=cost(6 * tokens * width * width, 8 * tokens * width + 6 * width * width))(x, w, q_gain, k_gain, cos_t, sin_t)


def out_proj_full(o_a, o_b, w, row_block, depth, x, gain):
    tokens, width = x.shape
    shards, tps, _, cols = w.shape
    half = depth // 2
    tr = min(256, tokens)

    def body(oa_ref, ob_ref, w_ref, x_ref, gain_ref, ha_ref, hb_ref, o_ref, raw_ref, sq_ref):
        f = pl.program_id(0)

        @pl.when(f == 0)
        def _():
            for t in range(tps):
                o_ref[:, t * depth:t * depth + half] = oa_ref[t]
                o_ref[:, t * depth + half:(t + 1) * depth] = ob_ref[t]

        out = dot(o_ref[...], w_ref[...].reshape(tps * depth, cols)).astype(BF16)
        raw_ref[f] = out
        out = out.astype(F32)
        sq_ref[...] = jnp.where(f == 0, 0.0, sq_ref[...]) + jnp.sum(out * out, axis=-1, keepdims=True)

        @pl.when(f == shards - 1)
        def _():
            def rows_body(r, _):
                rows = pl.ds(r * tr, tr)
                inv = lax.rsqrt(sq_ref[rows, :] / width + NORM_EPS)
                for m in range(shards):
                    c = slice(m * cols, (m + 1) * cols)
                    dst = slice(m // 2 * cols, (m // 2 + 1) * cols)
                    (ha_ref, hb_ref)[m % 2][rows, dst] = (
                        x_ref[rows, c].astype(F32) + raw_ref[m, rows, :].astype(F32) * inv * gain_ref[:, c]).astype(BF16)
                return 0

            lax.fori_loop(0, tokens // tr, rows_body, 0)

    fixed = lambda s: pl.BlockSpec(s, lambda f: (0,) * len(s), pipeline_mode=pl.Buffered(1))
    return pl.pallas_call(
        body, grid=(shards,),
        in_specs=[fixed(o_a.shape), fixed(o_b.shape), pl.BlockSpec((1, tps, depth, cols), lambda f: (f, 0, row_block, 0)),
                  fixed((tokens, width)), fixed((1, width))],
        out_specs=[pl.BlockSpec((tokens, width // 2), lambda f: (0, 0))] * 2,
        out_shape=[jax.ShapeDtypeStruct((tokens, width // 2), BF16)] * 2,
        scratch_shapes=[pltpu.VMEM((tokens, width), BF16), pltpu.VMEM((shards, tokens, cols), BF16), pltpu.VMEM((tokens, 1), F32)],
        compiler_params=params(),
        cost_estimate=cost(2 * tokens * width * width, 2 * width * (width + 2 * tokens)))(o_a, o_b, w, x, gain)


class Ring:
    def __init__(self, axis, size):
        assert size == 4
        self.axis, self.size = axis, size

    def up(self, a):
        return lax.ppermute(a, self.axis, [(i, (i + 1) % self.size) for i in range(self.size)])

    def down(self, a):
        return lax.ppermute(a, self.axis, [(i, (i - 1) % self.size) for i in range(self.size)])

    def gather(self, a, b):
        below_a, above_b = self.up(a), self.down(b)
        below_b, above_a = self.up(b), self.down(a)
        far_a, far_b = self.up(below_a), self.down(above_b)
        return [(a, b), (above_a, above_b), (far_a, far_b), (below_a, below_b)]

    def scatter(self, parts):
        own_a, own_b, one_a, one_b, two_a, two_b, three_a, three_b = parts
        far_a, far_b = self.up(two_a), self.down(two_b)
        below_b, above_a = self.up(one_b), self.down(three_a)
        below_a = self.up(one_a + far_a)
        above_b = self.down(three_b + far_b)
        return [own_a, below_a, above_a], [own_b, below_b, above_b]


def solution(mesh):
    cores = 2
    dp, tp, fsdp = mesh.shape['dp'], mesh.shape['tp'], mesh.shape['fsdp']
    xs = fsdp // cores
    mesh = jax.sharding.Mesh(mesh.devices.reshape(dp, tp, xs, cores), ('dp', 'tp', 'x', 'c'))
    shards = ('x', 'c')
    batch_axes = ('dp', 'x', 'c')
    act_spec = P(batch_axes, None, None)
    in_cols = P(None, shards, 'tp')
    in_rows = P(None, 'tp', shards)
    tp_gain = P(None, 'tp')
    fsdp_gain = P(None, shards)
    cache_spec = P(None, batch_axes, None, 'tp', None)
    ring_y, ring_x = Ring('tp', tp), Ring('x', xs)

    def gather_all(a):
        g = lax.all_gather(a, ('x', 'c', 'tp'), axis=0, tiled=False)
        return g.reshape(fsdp, tp, *a.shape)

    def blocks_of(w, cols):
        return [w[:, i:i + cols] for i in range(0, w.shape[1], cols)]

    def local_layers(x, w_query, w_key, w_value, w_out, w_gate, w_up, w_down, q_norm_w, k_norm_w, attn_norm_w, ffn_norm_w):
        batch, seq_len, width = x.shape
        assert batch == tp and w_query.shape[0] == 2
        tokens = batch * seq_len
        qc = seq_len // CHUNKS
        part = w_query.shape[2]
        cols = w_out.shape[2]
        ff = w_gate.shape[2]
        per_side = width // 2 // cols
        cos_t, sin_t = rope_tables(seq_len)
        me = lax.axis_index('tp')
        seq_order = lax.rem(me + jnp.arange(tp, dtype=jnp.int32), tp)

        w_qkv = lax.all_gather(jnp.concatenate([w_query[0], w_key[0], w_value[0]], axis=1), shards, axis=0, tiled=True)
        fsdp_gains = lax.all_gather(jnp.stack([attn_norm_w, ffn_norm_w]), shards, axis=2, tiled=True)
        tp_gains = lax.all_gather(jnp.stack([q_norm_w[1], k_norm_w[1]]), 'tp', axis=1, tiled=True)
        x, fsdp_gains, tp_gains = lax.optimization_barrier((x, fsdp_gains, tp_gains))
        w_o0 = gather_all(w_out[0])
        w_gu0 = lax.all_gather(jnp.concatenate([w_gate[0], w_up[0]], axis=1), shards, axis=0, tiled=True)
        w_d0 = lax.all_gather(w_down[0], shards, axis=0, tiled=False)
        w_attn1 = gather_all(jnp.concatenate(
            blocks_of(w_query[1], cols) + blocks_of(w_key[1], cols) + blocks_of(w_value[1], cols) + [w_out[1]], axis=0))
        share = ff // xs
        pieces = [jnp.concatenate(blocks_of(w_gate[1][:, i * share:(i + 1) * share], cols)
                                  + blocks_of(w_up[1][:, i * share:(i + 1) * share], cols)
                                  + [w_down[1][i * share:(i + 1) * share]], axis=0) for i in range(xs)]
        mlp1 = lax.all_to_all(jnp.stack(pieces), 'x', split_axis=0, concat_axis=0, tiled=True)
        mlp1 = lax.all_gather(mlp1, ('c', 'tp'), axis=0, tiled=False)
        mlp1 = mlp1.reshape(cores, tp, *mlp1.shape[1:])
        depth = w_gate.shape[1]
        up_rows = share // cols * depth

        q_raw, k_raw, values, sq = qkv_raw(x.reshape(tokens, width), w_qkv)
        sq_up, sq_down = ring_y.up(sq), ring_y.down(sq)
        sq_far = lax.ppermute(sq, 'tp', [(i, (i + 2) % tp) for i in range(tp)])
        inv = lax.rsqrt((sq + sq_up + sq_down + sq_far) / width + NORM_EPS)
        queries, keys_rot = norm_rope(q_raw, k_raw, inv, q_norm_w[:1], k_norm_w[:1], cos_t, sin_t)
        shape3 = (batch, seq_len, part)
        queries, keys_rot, values = (a.reshape(shape3) for a in (queries, keys_rot, values))

        def mlp(hs, w, gate, up, w_down, down, ff):
            steps = ff // 256 // 2
            acts = [mlp_up(hs, w, gate, up, i * steps, steps) for i in range(2)]
            return mlp_down(acts, w_down, down, len(hs), width)

        def cols_spec(offset):
            return lambda index: pl.BlockSpec((width, 256), lambda i: (0, offset + index(i)))

        gate0, up0 = cols_spec(0), cols_spec(ff // 256)
        down0 = lambda index: pl.BlockSpec((1, ff, cols), lambda i: (index(i), 0, 0))
        gathered = []
        for c in range(CHUNKS):
            own = attention(queries, c, qc, [(keys_rot, values, qc * (c + 1))])
            gathered.append(ring_y.gather(*own))
        sums, own_h = [], []
        for c in range(CHUNKS):
            outs = [a for pair in gathered[c] for a in pair]
            h_a, h_b = out_proj_gathered(seq_order, outs, w_o0, x, fsdp_gains[0, :1], c)
            sums.append(mlp([(h_a[s], h_b[s]) for s in range(batch)], w_gu0, gate0, up0, w_d0, down0, ff))
            own_h.append((h_a[0], h_b[0]))

        def up_spec(block):
            return lambda index: pl.BlockSpec((cores, 1, xs, depth, 256),
                                              lambda i: (0, index(i) // (share // 256), 0, block + index(i) % (share // 256), 0))

        gate1, up1 = up_spec(0), up_spec(share // 256)
        down1 = lambda index: pl.BlockSpec((1, tp, 1, share, cols), lambda i: (index(i) // xs, 0, index(i) % xs, 2 * up_rows // share, 0))
        kvs, caches, h1, gathered = [], [], [], []
        for c in range(CHUNKS):
            sum_a, sum_b = ring_y.scatter(sums[c])
            hidden, = finish(sum_a, sum_b, *own_h[c], fsdp_gains[1, :1], lambda side, b: side * per_side + b, True)
            q1, k1, v1 = qkv_full(hidden, w_attn1, tp_gains[:1], tp_gains[1:], cos_t, sin_t, part, c)
            caches.append([lax.all_to_all(a, 'tp', split_axis=0, concat_axis=0, tiled=True) for a in (k1, v1)])
            kvs.append((k1, v1, qc))
            own = attention(q1, 0, qc, list(kvs))
            h1.append(out_proj_full(*own, w_attn1, 3 * part * depth // cols // w_out.shape[1], w_out.shape[1], hidden,
                                    fsdp_gains[0, 1:]))
            gathered.append(ring_x.gather(*h1[-1]))
        sums = []
        for c in range(CHUNKS):
            hs = gathered[c]
            if c == CHUNKS - 1:
                hs, caches = lax.optimization_barrier((hs, caches))
            sums.append(mlp(hs, mlp1, gate1, up1, mlp1, down1, tp * share))
        y = jnp.zeros(x.shape, BF16)
        for c in range(CHUNKS):
            sum_a, sum_b = ring_x.scatter(sums[c])
            y_own = finish(sum_a, sum_b, *h1[c], fsdp_gains[1, 1:], lambda side, b: 2 * b + side, False)
            for rel, pair in enumerate(ring_y.gather(*y_own)):
                for side in range(2):
                    y = lax.dynamic_update_slice(y, pair[side][None], (seq_order[rel], c * qc, side * width // 2))

        def cache(first, n):
            second = jnp.concatenate([caches[c][n] for c in range(CHUNKS)], axis=1)
            return jnp.stack([first, second]).reshape(2, batch, seq_len, part // HEAD_DIM, HEAD_DIM)

        return y, cache(keys_rot, 0), cache(values, 1)

    return jax.shard_map(local_layers, mesh=mesh,
                         in_specs=(act_spec, in_cols, in_cols, in_cols, in_rows, in_cols, in_cols, in_rows,
                                   tp_gain, tp_gain, fsdp_gain, fsdp_gain),
                         out_specs=(act_spec, cache_spec, cache_spec), check_vma=False)
```

profile of v0, /device:TPU:96, one launch (start us, length us, event | category | flops | bytes accessed | tf_op | source)
XLA Modules:
  0.0 1267.6 jit_solution(4835882881751594343)
XLA Ops:
  27.3 57.6 %all_to_all.25 = bf16[4,1536,256]{2,1,0:T(8,128)(2,1)} all-to-all(bf16[4,1536,256]{2,1,0:T(8,128)(2,1)S(1)} %pad_maximum_fusion.4), channel_id=1, replica_groups=mesh['dp'=1,'tp'=4,'x'=4,'c'=2] {'x'}, dimensions={0} | all-to-all | bytes 6291456 | tf_op jit(solution)/shard_map/all_to_all | solution.py:469
  85.5 12.4 all_gather.31
  98.0 22.2 %all_gather.30 = f32[2,2,2048]{2,1,0:T(2,128)S(1)} all-gather(f32[2,2,256]{2,1,0:T(2,128)S(1)} %pad_maximum_fusion.9), channel_id=1, replica_groups=mesh['dp'=1,'tp'=4,'x'=4,'c'=2] {'x','c'}, dimensions={2}, use_global_device_ids=true | all-gather | bytes 36864 | tf_op jit(solution)/shard_map/all_gather | solution.py:457
  122.1 32.1 %qkv_raw.1 = (f32[4096,512]{1,0:T(8,128)}, f32[4096,512]{1,0:T(8,128)}, bf16[4096,512]{1,0:T(8,128)(2,1)}, f32[8,4096]{1,0:T(8,128)}) custom-call(bf16[4096,2048]{1,0:T(8,128)(2,1)} %bitcast.143, bf16[2048,1536]{1,0:T(8,128)(2,1)} %all-gather.9.cloned.1.call-done.w_ref), custom_call_target="tpu_custom_call" | custom-call | flops 25769803776 | bytes 37748736 | tf_op jit(solution)/shard_map/qkv_raw/pallas_call | solution.py:60
  166.0 13.6 %norm_rope.1 = (bf16[4096,512]{1,0:T(8,128)(2,1)}, bf16[4096,512]{1,0:T(8,128)(2,1)}) custom-call(f32[4096,512]{1,0:T(8,128)} %get-tuple-element.83.q_ref, f32[4096,512]{1,0:T(8,128)} %get-tuple-element.84.k_ref, f32[8,4096]{1,0:T(8,128)} %add_rsqrt_fusion.inv_ref, f32[1,512]{1,0:T(1,128)} %get-tuple-element.225.qg_ref, f32[1,512]{1,0:T(1,128)} %get-tuple-element.213.kg_ref, ...), custom_call_target="tpu_custom_call" | custom-call | flops 4194304000 | bytes 25165824 | tf_op jit(solution)/shard_map/norm_rope/pallas_call | solution.py:86
  179.6 22.3 %shard_map.152 = (bf16[4,512,256]{2,1,0:T(8,128)(2,1)}, bf16[4,512,256]{2,1,0:T(8,128)(2,1)}) custom-call(bf16[4,1024,512]{2,1,0:T(8,128)(2,1)} %bitcast.146, bf16[4,1024,512]{2,1,0:T(8,128)(2,1)} %bitcast.125, bf16[4,1024,512]{2,1,0:T(8,128)(2,1)} %bitcast.123), custom_call_target="tpu_custom_call" | custom-call | flops 8589934592 | bytes 12582912 | tf_op jit(solution)/shard_map/pallas_call | solution.py:138
  207.2 15.7 %shard_map.139 = (bf16[4,512,256]{2,1,0:T(8,128)(2,1)}, bf16[4,512,256]{2,1,0:T(8,128)(2,1)}) custom-call(bf16[4,1024,512]{2,1,0:T(8,128)(2,1)} %bitcast.147, bf16[4,1024,512]{2,1,0:T(8,128)(2,1)} %bitcast.126, bf16[4,1024,512]{2,1,0:T(8,128)(2,1)} %bitcast.124), custom_call_target="tpu_custom_call" | custom-call | flops 4294967296 | bytes 8388608 | tf_op jit(solution)/shard_map/pallas_call | solution.py:138
  232.4 19.1 %collective-permute-done.33.refs_2_ = bf16[4,512,256]{2,1,0:T(8,128)(2,1)} collective-permute-done((bf16[4,512,256]{2,1,0:T(8,128)(2,1)}, bf16[4,512,256]{2,1,0:T(8,128)(2,1)}, u32[]{:S(2)}, u32[]{:S(2)}) %collective-permute-start.33) | collective-permute-done | bytes 1048608 | tf_op jit(solution)/shard_map/ppermute | solution.py:404
  257.1 17.3 %collective-permute-done.5.refs_6_ = bf16[4,512,256]{2,1,0:T(8,128)(2,1)S(1)} collective-permute-done((bf16[4,512,256]{2,1,0:T(8,128)(2,1)}, bf16[4,512,256]{2,1,0:T(8,128)(2,1)S(1)}, u32[]{:S(2)}, u32[]{:S(2)}) %collective-permute-start.5) | collective-permute-done | bytes 1048608 | tf_op jit(solution)/shard_map/ppermute | solution.py:401
  274.5 39.3 %collective-permute-done.36.refs_4_ = bf16[4,512,256]{2,1,0:T(8,128)(2,1)} collective-permute-done((bf16[4,512,256]{2,1,0:T(8,128)(2,1)}, bf16[4,512,256]{2,1,0:T(8,128)(2,1)}, u32[]{:S(2)}, u32[]{:S(2)}) %collective-permute-start.36) | collective-permute-done | bytes 1048608 | tf_op jit(solution)/shard_map/ppermute | solution.py:401
  314.6 31.6 %shard_map.153 = (bf16[4,512,1024]{2,1,0:T(8,128)(2,1)}, bf16[4,512,1024]{2,1,0:T(8,128)(2,1)}) custom-call(s32[4]{0:T(128)} %compare_select_fusion.order_ref, bf16[4,512,256]{2,1,0:T(8,128)(2,1)} %get-tuple-element.120.refs_0_, bf16[4,512,256]{2,1,0:T(8,128)(2,1)} %get-tuple-element.121.refs_1_, bf16[4,512,256]{2,1,0:T(8,128)(2,1)} %collective-permute-done.33.refs_2_, ...), custom_call_target="tpu_custom_call" | custom-call | flops 17179869184 | bytes 33554432 | tf_op jit(solution)/shard_map/pallas_call | solution.py:173
  354.1 34.7 %collective-permute-done.6.refs_4_ = bf16[4,512,256]{2,1,0:T(8,128)(2,1)} collective-permute-done((bf16[4,512,256]{2,1,0:T(8,128)(2,1)S(1)}, bf16[4,512,256]{2,1,0:T(8,128)(2,1)}, u32[]{:S(2)}, u32[]{:S(2)}) %collective-permute-start.6) | collective-permute-done | bytes 1048608 | tf_op jit(solution)/shard_map/ppermute | solution.py:401
  391.0 29.2 %shard_map.140 = (bf16[4,512,1024]{2,1,0:T(8,128)(2,1)}, bf16[4,512,1024]{2,1,0:T(8,128)(2,1)}) custom-call(s32[4]{0:T(128)} %compare_select_fusion.order_ref, bf16[4,512,256]{2,1,0:T(8,128)(2,1)} %get-tuple-element.89.refs_0_, bf16[4,512,256]{2,1,0:T(8,128)(2,1)} %get-tuple-element.90.refs_1_, bf16[4,512,256]{2,1,0:T(8,128)(2,1)} %collective-permute-done.3.refs_2_, ...), custom_call_target="tpu_custom_call" | custom-call | flops 17179869184 | bytes 33554432 | tf_op jit(solution)/shard_map/pallas_call | solution.py:173
  426.8 25.0 %shard_map.155.refs_1_ = bf16[2048,1024]{1,0:T(8,128)(2,1)} custom-call(bf16[512,1024]{1,0:T(8,128)(2,1)} %get-tuple-element.168.refs_0_.refs_6_, bf16[512,1024]{1,0:T(8,128)(2,1)} %get-tuple-element.164.refs_1_.refs_7_, bf16[512,1024]{1,0:T(8,128)(2,1)} %get-tuple-element.167.refs_2_, bf16[512,1024]{1,0:T(8,128)(2,1)} %get-tuple-element.163.refs_3_, ...), custom_call_target="tpu_custom_call" | custom-call | flops 17179869184 | bytes 16777216 | tf_op jit(solution)/shard_map/pallas_call | solution.py:207
  451.8 23.5 %shard_map.154.refs_0_ = bf16[2048,1024]{1,0:T(8,128)(2,1)} custom-call(bf16[512,1024]{1,0:T(8,128)(2,1)} %get-tuple-element.168.refs_0_.refs_6_, bf16[512,1024]{1,0:T(8,128)(2,1)} %get-tuple-element.164.refs_1_.refs_7_, bf16[512,1024]{1,0:T(8,128)(2,1)} %get-tuple-element.167.refs_2_, bf16[512,1024]{1,0:T(8,128)(2,1)} %get-tuple-element.163.refs_3_, ...), custom_call_target="tpu_custom_call" | custom-call | flops 17179869184 | bytes 16777216 | tf_op jit(solution)/shard_map/pallas_call | solution.py:207
  475.3 24.9 %shard_map.156 = (bf16[512,1024]{1,0:T(8,128)(2,1)}, bf16[512,1024]{1,0:T(8,128)(2,1)}, bf16[512,1024]{1,0:T(8,128)(2,1)}, bf16[512,1024]{1,0:T(8,128)(2,1)}, bf...) custom-call(bf16[2048,1024]{1,0:T(8,128)(2,1)} %shard_map.154.refs_0, ...), custom_call_target="tpu_custom_call" | custom-call | flops 17179869184 | bytes 25165824 | tf_op jit(solution)/shard_map/pallas_call | solution.py:245
  507.9 23.4 %shard_map.142.refs_1_ = bf16[2048,1024]{1,0:T(8,128)(2,1)} custom-call(bf16[512,1024]{1,0:T(8,128)(2,1)} %get-tuple-element.176.refs_0_.refs_6_, bf16[512,1024]{1,0:T(8,128)(2,1)} %get-tuple-element.172.refs_1_.refs_7_, bf16[512,1024]{1,0:T(8,128)(2,1)} %get-tuple-element.175.refs_2_, bf16[512,1024]{1,0:T(8,128)(2,1)} %get-tuple-element.171.refs_3_, ...), custom_call_target="tpu_custom_call" | custom-call | flops 17179869184 | bytes 16777216 | tf_op jit(solution)/shard_map/pallas_call | solution.py:207
  531.4 23.4 %shard_map.141.refs_0_ = bf16[2048,1024]{1,0:T(8,128)(2,1)} custom-call(bf16[512,1024]{1,0:T(8,128)(2,1)} %get-tuple-element.176.refs_0_.refs_6_, bf16[512,1024]{1,0:T(8,128)(2,1)} %get-tuple-element.172.refs_1_.refs_7_, bf16[512,1024]{1,0:T(8,128)(2,1)} %get-tuple-element.175.refs_2_, bf16[512,1024]{1,0:T(8,128)(2,1)} %get-tuple-element.171.refs_3_, ...), custom_call_target="tpu_custom_call" | custom-call | flops 17179869184 | bytes 16777216 | tf_op jit(solution)/shard_map/pallas_call | solution.py:207
  563.6 25.1 %shard_map.143 = (bf16[512,1024]{1,0:T(8,128)(2,1)}, bf16[512,1024]{1,0:T(8,128)(2,1)}, bf16[512,1024]{1,0:T(8,128)(2,1)}, bf16[512,1024]{1,0:T(8,128)(2,1)}, bf...) custom-call(bf16[2048,1024]{1,0:T(8,128)(2,1)} %shard_map.141.refs_0, ...), custom_call_target="tpu_custom_call" | custom-call | flops 17179869184 | bytes 25165824 | tf_op jit(solution)/shard_map/pallas_call | solution.py:245
  592.0 21.2 %collective-permute-done.44.refs_5_ = bf16[512,1024]{1,0:T(8,128)(2,1)S(1)} collective-permute-done((bf16[512,1024]{1,0:T(8,128)(2,1)}, bf16[512,1024]{1,0:T(8,128)(2,1)S(1)}, u32[]{:S(2)}, u32[]{:S(2)}) %collective-permute-start.44) | collective-permute-done | bytes 1048608 | tf_op jit(solution)/shard_map/ppermute | solution.py:404
  620.0 32.8 %shard_map.158 = (bf16[4,512,512]{2,1,0:T(8,128)(2,1)}, bf16[4,512,512]{2,1,0:T(8,128)(2,1)}, bf16[4,512,512]{2,1,0:T(8,128)(2,1)}) custom-call(bf16[512,2048]{1,0:T(8,128)(2,1)} %shard_map.157.x_ref, bf16[8,4,2048,256]{3,2,1,0:T(8,128)(2,1)} %bitcast.119, f32[1,2048]{1,0:T(1,128)} %get-tuple-element.212.qg_ref, f32[1,2048]{1,0:T(1,128)} %get-tuple-element.211.kg_ref, ...), custom_call_target="tpu_custom_call" | custom-call | flops 12884901888 | bytes 33554432 | tf_op jit(solution)/shard_map/pallas_call | solution.py:337
  669.0 15.8 %all-to-all-done.3 = bf16[4,512,512]{2,1,0:T(8,128)(2,1)S(1)} async-done(((bf16[4,512,512]{2,1,0:T(8,128)(2,1)}), bf16[4,512,512]{2,1,0:T(8,128)(2,1)S(1)}, u32[]{:S(2)}, u32[]{:S(2)}) %all-to-all-start.3) | async-done | bytes 2097184 | tf_op jit(solution)/shard_map/all_to_all | solution.py:515
  689.4 16.5 %collective-permute-done.11.refs_2_ = bf16[512,1024]{1,0:T(8,128)(2,1)} collective-permute-done((bf16[512,1024]{1,0:T(8,128)(2,1)}, bf16[512,1024]{1,0:T(8,128)(2,1)}, u32[]{:S(2)}, u32[]{:S(2)}) %collective-permute-start.11) | collective-permute-done | bytes 1048608 | tf_op jit(solution)/shard_map/ppermute | solution.py:404
  705.9 16.9 %collective-permute-done.14.refs_5_ = bf16[512,1024]{1,0:T(8,128)(2,1)} collective-permute-done((bf16[512,1024]{1,0:T(8,128)(2,1)}, bf16[512,1024]{1,0:T(8,128)(2,1)}, u32[]{:S(2)}, u32[]{:S(2)}) %collective-permute-start.14) | collective-permute-done | bytes 1048608 | tf_op jit(solution)/shard_map/ppermute | solution.py:404
  729.4 32.7 %shard_map.145 = (bf16[4,512,512]{2,1,0:T(8,128)(2,1)}, bf16[4,512,512]{2,1,0:T(8,128)(2,1)}, bf16[4,512,512]{2,1,0:T(8,128)(2,1)}) custom-call(bf16[512,2048]{1,0:T(8,128)(2,1)} %shard_map.144.x_ref, bf16[8,4,2048,256]{3,2,1,0:T(8,128)(2,1)} %bitcast.120, f32[1,2048]{1,0:T(1,128)} %get-tuple-element.212.qg_ref, f32[1,2048]{1,0:T(1,128)} %get-tuple-element.211.kg_ref, ...), custom_call_target="tpu_custom_call" | custom-call | flops 12884901888 | bytes 33554432 | tf_op jit(solution)/shard_map/pallas_call | solution.py:337
  766.0 22.3 %shard_map.159 = (bf16[4,512,256]{2,1,0:T(8,128)(2,1)}, bf16[4,512,256]{2,1,0:T(8,128)(2,1)}) custom-call(bf16[4,512,512]{2,1,0:T(8,128)(2,1)} %get-tuple-element.132.q_ref, bf16[4,512,512]{2,1,0:T(8,128)(2,1)} %get-tuple-element.104.refs_0_, bf16[4,512,512]{2,1,0:T(8,128)(2,1)} %get-tuple-element.133.refs_1_, ...), custom_call_target="tpu_custom_call" | custom-call | flops 8589934592 | bytes 12582912 | tf_op jit(solution)/shard_map/pallas_call | solution.py:138
  788.2 13.1 %shard_map.160 = (bf16[512,1024]{1,0:T(8,128)(2,1)}, bf16[512,1024]{1,0:T(8,128)(2,1)}) custom-call(bf16[4,512,256]{2,1,0:T(8,128)(2,1)} %get-tuple-element.135.oa_ref, bf16[4,512,256]{2,1,0:T(8,128)(2,1)} %get-tuple-element.136.ob_ref, bf16[8,4,2048,256]{3,2,1,0:T(8,128)(2,1)} %bitcast.121, bf16[512,2048]{1,0:T(8,128)(2,1)} %shard_map.157.x_ref, ...), custom_call_target="tpu_custom_call" | custom-call | flops 4294967296 | bytes 12582912 | tf_op jit(solution)/shard_map/pallas_call | solution.py:384
  811.3 15.5 %shard_map.146 = (bf16[4,512,256]{2,1,0:T(8,128)(2,1)}, bf16[4,512,256]{2,1,0:T(8,128)(2,1)}) custom-call(bf16[4,512,512]{2,1,0:T(8,128)(2,1)} %get-tuple-element.103.q_ref, bf16[4,512,512]{2,1,0:T(8,128)(2,1)} %get-tuple-element.104.refs_0_, bf16[4,512,512]{2,1,0:T(8,128)(2,1)} %get-tuple-element.105.refs_1_.refs_2_), custom_call_target="tpu_custom_call" | custom-call | flops 4294967296 | bytes 8388608 | tf_op jit(solution)/shard_map/pallas_call | solution.py:138
  826.8 13.0 %shard_map.147 = (bf16[512,1024]{1,0:T(8,128)(2,1)}, bf16[512,1024]{1,0:T(8,128)(2,1)}) custom-call(bf16[4,512,256]{2,1,0:T(8,128)(2,1)} %get-tuple-element.106.oa_ref, bf16[4,512,256]{2,1,0:T(8,128)(2,1)} %get-tuple-element.107.ob_ref, bf16[8,4,2048,256]{3,2,1,0:T(8,128)(2,1)} %bitcast.122, bf16[512,2048]{1,0:T(8,128)(2,1)} %shard_map.144.x_ref, ...), custom_call_target="tpu_custom_call" | custom-call | flops 4294967296 | bytes 12582912 | tf_op jit(solution)/shard_map/pallas_call | solution.py:384
  846.5 20.9 %collective-permute-done.17.refs_6_ = bf16[512,1024]{1,0:T(8,128)(2,1)S(1)} collective-permute-done((bf16[512,1024]{1,0:T(8,128)(2,1)}, bf16[512,1024]{1,0:T(8,128)(2,1)S(1)}, u32[]{:S(2)}, u32[]{:S(2)}) %collective-permute-start.17) | collective-permute-done | bytes 1048608 | tf_op jit(solution)/shard_map/ppermute | solution.py:401
  867.8 22.0 %collective-permute-done.48.refs_4_ = bf16[512,1024]{1,0:T(8,128)(2,1)S(1)} collective-permute-done((bf16[512,1024]{1,0:T(8,128)(2,1)S(1)}, bf16[512,1024]{1,0:T(8,128)(2,1)S(1)}, u32[]{:S(2)}, u32[]{:S(2)}) %collective-permute-start.48) | collective-permute-done | bytes 1048608 | tf_op jit(solution)/shard_map/ppermute | solution.py:401
  891.9 23.6 %shard_map.162.refs_1_ = bf16[2048,1024]{1,0:T(8,128)(2,1)} custom-call(bf16[512,1024]{1,0:T(8,128)(2,1)} %get-tuple-element.139.refs_0_.refs_6_, bf16[512,1024]{1,0:T(8,128)(2,1)} %get-tuple-element.140.refs_1_.refs_7_, bf16[512,1024]{1,0:T(8,128)(2,1)} %collective-permute-done.45.refs_2_, bf16[512,1024]{1,0:T(8,128)(2,1)} %collective-permute-done.46.refs_3_, ...), custom_call_target="tpu_custom_call" | custom-call | flops 17179869184 | bytes 16777216 | tf_op jit(solution)/shard_map/pallas_call | solution.py:207
  915.5 23.4 %shard_map.161.refs_0_ = bf16[2048,1024]{1,0:T(8,128)(2,1)} custom-call(bf16[512,1024]{1,0:T(8,128)(2,1)} %get-tuple-element.139.refs_0_.refs_6_, bf16[512,1024]{1,0:T(8,128)(2,1)} %get-tuple-element.140.refs_1_.refs_7_, bf16[512,1024]{1,0:T(8,128)(2,1)} %collective-permute-done.45.refs_2_, bf16[512,1024]{1,0:T(8,128)(2,1)} %collective-permute-done.46.refs_3_, ...), custom_call_target="tpu_custom_call" | custom-call | flops 17179869184 | bytes 16777216 | tf_op jit(solution)/shard_map/pallas_call | solution.py:207
  938.9 23.3 %shard_map.149.refs_1_ = bf16[2048,1024]{1,0:T(8,128)(2,1)} custom-call(bf16[512,1024]{1,0:T(8,128)(2,1)} %get-tuple-element.108.refs_0_.refs_6_, bf16[512,1024]{1,0:T(8,128)(2,1)} %get-tuple-element.109.refs_1_.refs_7_, bf16[512,1024]{1,0:T(8,128)(2,1)} %collective-permute-done.15.refs_2_, bf16[512,1024]{1,0:T(8,128)(2,1)} %copy-done.40, ...), custom_call_target="tpu_custom_call" | custom-call | flops 17179869184 | bytes 16777216 | tf_op jit(solution)/shard_map/pallas_call | solution.py:207
  962.2 23.3 %shard_map.148.refs_0_ = bf16[2048,1024]{1,0:T(8,128)(2,1)} custom-call(bf16[512,1024]{1,0:T(8,128)(2,1)} %get-tuple-element.108.refs_0_.refs_6_, bf16[512,1024]{1,0:T(8,128)(2,1)} %get-tuple-element.109.refs_1_.refs_7_, bf16[512,1024]{1,0:T(8,128)(2,1)} %collective-permute-done.15.refs_2_, bf16[512,1024]{1,0:T(8,128)(2,1)} %copy-done.40, ...), custom_call_target="tpu_custom_call" | custom-call | flops 17179869184 | bytes 16777216 | tf_op jit(solution)/shard_map/pallas_call | solution.py:207
  985.4 25.4 %shard_map.150 = (bf16[512,1024]{1,0:T(8,128)(2,1)}, bf16[512,1024]{1,0:T(8,128)(2,1)}, bf16[512,1024]{1,0:T(8,128)(2,1)}, bf16[512,1024]{1,0:T(8,128)(2,1)}, bf...) custom-call(bf16[2048,1024]{1,0:T(8,128)(2,1)} %shard_map.148.refs_0, ...), custom_call_target="tpu_custom_call" | custom-call | flops 17179869184 | bytes 25165824 | tf_op jit(solution)/shard_map/pallas_call | solution.py:245
  1012.9 25.0 %shard_map.163 = (bf16[512,1024]{1,0:T(8,128)(2,1)}, bf16[512,1024]{1,0:T(8,128)(2,1)}, bf16[512,1024]{1,0:T(8,128)(2,1)}, bf16[512,1024]{1,0:T(8,128)(2,1)}, bf...) custom-call(bf16[2048,1024]{1,0:T(8,128)(2,1)} %shard_map.161.refs_0, ...), custom_call_target="tpu_custom_call" | custom-call | flops 17179869184 | bytes 25165824 | tf_op jit(solution)/shard_map/pallas_call | solution.py:245
  1051.7 7.0 stack.55
  1070.1 7.0 stack.56
  1081.0 7.0 stack.53
  1097.1 8.8 pad_maximum_fusion.1
  1110.1 18.8 %collective-permute-done.24.refs_4_ = bf16[512,1024]{1,0:T(8,128)(2,1)S(1)} collective-permute-done((bf16[512,1024]{1,0:T(8,128)(2,1)S(1)}, bf16[512,1024]{1,0:T(8,128)(2,1)S(1)}, u32[]{:S(2)}, u32[]{:S(2)}) %collective-permute-start.24) | collective-permute-done | bytes 1048608 | tf_op jit(solution)/shard_map/ppermute | solution.py:401
  1131.0 9.2 collective-permute-done.22.refs_1_
  1153.4 8.7 pad_maximum_fusion
  1170.5 7.2 collective-permute-done.29
  1179.9 15.0 %collective-permute-done.28 = bf16[512,1024]{1,0:T(8,128)(2,1)} collective-permute-done((bf16[512,1024]{1,0:T(8,128)(2,1)}, bf16[512,1024]{1,0:T(8,128)(2,1)}, u32[]{:S(2)}, u32[]{:S(2)}) %collective-permute-start.28) | collective-permute-done | bytes 1048608 | tf_op jit(solution)/shard_map/ppermute | solution.py:404
  1201.6 18.6 %collective-permute-done.30 = bf16[512,1024]{1,0:T(8,128)(2,1)S(1)} collective-permute-done((bf16[512,1024]{1,0:T(8,128)(2,1)}, bf16[512,1024]{1,0:T(8,128)(2,1)S(1)}, u32[]{:S(2)}, u32[]{:S(2)}) %collective-permute-start.30) | collective-permute-done | bytes 1048608 | tf_op jit(solution)/shard_map/ppermute | solution.py:401
  1235.2 18.6 %collective-permute-done.60 = bf16[512,1024]{1,0:T(8,128)(2,1)S(1)} collective-permute-done((bf16[512,1024]{1,0:T(8,128)(2,1)S(1)}, bf16[512,1024]{1,0:T(8,128)(2,1)S(1)}, u32[]{:S(2)}, u32[]{:S(2)}) %collective-permute-start.60) | collective-permute-done | bytes 1048608 | tf_op jit(solution)/shard_map/ppermute | solution.py:401
  (287 shorter events, 240.4 us)
Async XLA Ops:
  7.2 114.9 %all-gather.9.cloned.1.call-start = ((), (), s32[]{:S(2)}) async-start(), calls=%async_computation.5 | async-start | bytes 7077888 | tf_op jit(solution)/shard_map/all_gather | solution.py:456
  11.4 303.1 %all-gather.11.cloned.1.call-start = ((), (), s32[]{:S(2)}) async-start(), calls=%async_computation.6 | async-start | bytes 8650752 | tf_op jit(solution)/shard_map/all_gather | solution.py:437
  12.3 414.5 %all-gather.13.cloned.1.call-start = ((), (), s32[]{:S(2)}) async-start(), calls=%async_computation.7 | async-start | bytes 18874368 | tf_op jit(solution)/shard_map/all_gather | solution.py:461
  16.6 458.7 %all-gather.15.cloned.1.call-start = ((), (), s32[]{:S(2)}) async-start(), calls=%async_computation.8 | async-start | bytes 9437184 | tf_op jit(solution)/shard_map/all_gather | solution.py:462
  19.0 600.9 %all-gather.17.cloned.1.call-start = ((), (), s32[]{:S(2)}) async-start(), calls=%async_computation.9 | async-start | bytes 34603008 | tf_op jit(solution)/shard_map/all_gather | solution.py:437
  25.0 866.8 %all-gather.19.cloned.1.call-start = ((), (), s32[]{:S(2)}) async-start(), calls=%async_computation.10 | async-start | bytes 28311552 | tf_op jit(solution)/shard_map/all_gather | solution.py:470
  205.2 46.3 %collective-permute-start.33 = (bf16[4,512,256]{2,1,0:T(8,128)(2,1)}, bf16[4,512,256]{2,1,0:T(8,128)(2,1)}, u32[]{:S(2)}, u32[]{:S(2)}) collective-permute-start(bf16[4,512,256]{2,1,0:T(8,128)(2,1)} %get-tuple-element.120.refs_0_), channel_id=1, source_target_pairs={{0,24},{8,0},{16,8},{24,16},{1,25},{9,1},{17,9},{25,17},{2,26},{10... | collective-permute-start | bytes 3145736 | tf_op jit(solution)/shard_map/ppermute | solution.py:404
  205.5 51.6 %collective-permute-start.38 = (bf16[4,512,256]{2,1,0:T(8,128)(2,1)}, bf16[4,512,256]{2,1,0:T(8,128)(2,1)}, u32[]{:S(2)}, u32[]{:S(2)}) collective-permute-start(bf16[4,512,256]{2,1,0:T(8,128)(2,1)} %get-tuple-element.121.refs_1_), channel_id=1, source_target_pairs={{0,8},{8,16},{16,24},{24,0},{1,9},{9,17},{17,25},{25,1},{2,10},{10... | collective-permute-start | bytes 3145736 | tf_op jit(solution)/shard_map/ppermute | solution.py:401
  222.9 51.5 %collective-permute-start.5 = (bf16[4,512,256]{2,1,0:T(8,128)(2,1)}, bf16[4,512,256]{2,1,0:T(8,128)(2,1)S(1)}, u32[]{:S(2)}, u32[]{:S(2)}) collective-permute-start(bf16[4,512,256]{2,1,0:T(8,128)(2,1)} %get-tuple-element.89.refs_0_), channel_id=1, source_target_pairs={{0,8},{8,16},{16,24},{24,0},{1,9},{9,17},{17,25},{25,1},{2,10},{10... | collective-permute-start | bytes 3145736 | tf_op jit(solution)/shard_map/ppermute | solution.py:401
  230.4 44.0 %collective-permute-start.4 = (bf16[4,512,256]{2,1,0:T(8,128)(2,1)}, bf16[4,512,256]{2,1,0:T(8,128)(2,1)S(1)}, u32[]{:S(2)}, u32[]{:S(2)}) collective-permute-start(bf16[4,512,256]{2,1,0:T(8,128)(2,1)} %get-tuple-element.90.refs_1_), channel_id=1, source_target_pairs={{0,24},{8,0},{16,8},{24,16},{1,25},{9,1},{17,9},{25,17},{2,26},{10... | collective-permute-start | bytes 3145736 | tf_op jit(solution)/shard_map/ppermute | solution.py:404
  230.6 83.1 %collective-permute-start.36 = (bf16[4,512,256]{2,1,0:T(8,128)(2,1)}, bf16[4,512,256]{2,1,0:T(8,128)(2,1)}, u32[]{:S(2)}, u32[]{:S(2)}) collective-permute-start(bf16[4,512,256]{2,1,0:T(8,128)(2,1)} %copy-done.38), channel_id=1, source_target_pairs={{0,8},{8,16},{16,24},{24,0},{1,9},{9,17},{17,25},{25,1},{2,10},{10... | collective-permute-start | bytes 3145736 | tf_op jit(solution)/shard_map/ppermute | solution.py:401
  251.5 63.0 %collective-permute-start.37 = (bf16[4,512,256]{2,1,0:T(8,128)(2,1)}, bf16[4,512,256]{2,1,0:T(8,128)(2,1)}, u32[]{:S(2)}, u32[]{:S(2)}) collective-permute-start(bf16[4,512,256]{2,1,0:T(8,128)(2,1)} %collective-permute-done.34.refs_3_), channel_id=1, source_target_pairs={{0,24},{8,0},{16,8},{24,16},{1,25},{9,1},{17,9},{25,17},{2,26},{10... | collective-permute-start | bytes 3145736 | tf_op jit(solution)/shard_map/ppermute | solution.py:404
  257.1 97.1 %collective-permute-start.3 = (bf16[4,512,256]{2,1,0:T(8,128)(2,1)}, bf16[4,512,256]{2,1,0:T(8,128)(2,1)}, u32[]{:S(2)}, u32[]{:S(2)}) collective-permute-start(bf16[4,512,256]{2,1,0:T(8,128)(2,1)} %get-tuple-element.89.refs_0_), channel_id=1, source_target_pairs={{0,24},{8,0},{16,8},{24,16},{1,25},{9,1},{17,9},{25,17},{2,26},{10... | collective-permute-start | bytes 3145736 | tf_op jit(solution)/shard_map/ppermute | solution.py:404
  274.4 79.8 %collective-permute-start.8 = (bf16[4,512,256]{2,1,0:T(8,128)(2,1)}, bf16[4,512,256]{2,1,0:T(8,128)(2,1)}, u32[]{:S(2)}, u32[]{:S(2)}) collective-permute-start(bf16[4,512,256]{2,1,0:T(8,128)(2,1)} %get-tuple-element.90.refs_1_), channel_id=1, source_target_pairs={{0,8},{8,16},{16,24},{24,0},{1,9},{9,17},{17,25},{25,1},{2,10},{10... | collective-permute-start | bytes 3145736 | tf_op jit(solution)/shard_map/ppermute | solution.py:401
  274.4 114.5 %collective-permute-start.6 = (bf16[4,512,256]{2,1,0:T(8,128)(2,1)S(1)}, bf16[4,512,256]{2,1,0:T(8,128)(2,1)}, u32[]{:S(2)}, u32[]{:S(2)}) collective-permute-start(bf16[4,512,256]{2,1,0:T(8,128)(2,1)S(1)} %collective-permute-done.5.refs_6_), channel_id=1, source_target_pairs={{0,8},{8,16},{16,24},{24,0},{1,9},{9,17},{17,25},{25,1},{2,10},{10... | collective-permute-start | bytes 3145736 | tf_op jit(solution)/shard_map/ppermute | solution.py:401
  313.8 77.2 %collective-permute-start.7 = (bf16[4,512,256]{2,1,0:T(8,128)(2,1)S(1)}, bf16[4,512,256]{2,1,0:T(8,128)(2,1)}, u32[]{:S(2)}, u32[]{:S(2)}) collective-permute-start(bf16[4,512,256]{2,1,0:T(8,128)(2,1)S(1)} %collective-permute-done.4.refs_3_), channel_id=1, source_target_pairs={{0,24},{8,0},{16,8},{24,16},{1,25},{9,1},{17,9},{25,17},{2,26},{10... | collective-permute-start | bytes 3145736 | tf_op jit(solution)/shard_map/ppermute | solution.py:404
  500.2 54.5 %collective-permute-start.43 = (bf16[512,1024]{1,0:T(8,128)(2,1)}, bf16[512,1024]{1,0:T(8,128)(2,1)}, u32[]{:S(2)}, u32[]{:S(2)}) collective-permute-start(bf16[512,1024]{1,0:T(8,128)(2,1)} %get-tuple-element.131), channel_id=1, source_target_pairs={{0,24},{8,0},{16,8},{24,16},{1,25},{9,1},{17,9},{25,17},{2,26},{10... | collective-permute-start | bytes 3145736 | tf_op jit(solution)/shard_map/ppermute | solution.py:404
  504.7 56.0 %collective-permute-start.39 = (bf16[512,1024]{1,0:T(8,128)(2,1)}, bf16[512,1024]{1,0:T(8,128)(2,1)}, u32[]{:S(2)}, u32[]{:S(2)}) collective-permute-start(bf16[512,1024]{1,0:T(8,128)(2,1)} %get-tuple-element.126), channel_id=1, source_target_pairs={{0,8},{8,16},{16,24},{24,0},{1,9},{9,17},{17,25},{25,1},{2,10},{10... | collective-permute-start | bytes 3145736 | tf_op jit(solution)/shard_map/ppermute | solution.py:401
  504.7 87.3 %collective-permute-start.41 = (bf16[512,1024]{1,0:T(8,128)(2,1)}, bf16[512,1024]{1,0:T(8,128)(2,1)S(1)}, u32[]{:S(2)}, u32[]{:S(2)}) collective-permute-start(bf16[512,1024]{1,0:T(8,128)(2,1)} %get-tuple-element.127), channel_id=1, source_target_pairs={{0,24},{8,0},{16,8},{24,16},{1,25},{9,1},{17,9},{25,17},{2,26},{10... | collective-permute-start | bytes 3145736 | tf_op jit(solution)/shard_map/ppermute | solution.py:404
  507.9 84.1 %collective-permute-start.42 = (bf16[512,1024]{1,0:T(8,128)(2,1)}, bf16[512,1024]{1,0:T(8,128)(2,1)S(1)}, u32[]{:S(2)}, u32[]{:S(2)}) collective-permute-start(bf16[512,1024]{1,0:T(8,128)(2,1)} %get-tuple-element.129), channel_id=1, source_target_pairs={{0,8},{8,16},{16,24},{24,0},{1,9},{9,17},{17,25},{25,1},{2,10},{10... | collective-permute-start | bytes 3145736 | tf_op jit(solution)/shard_map/ppermute | solution.py:401
  557.4 55.8 %collective-permute-start.44 = (bf16[512,1024]{1,0:T(8,128)(2,1)}, bf16[512,1024]{1,0:T(8,128)(2,1)S(1)}, u32[]{:S(2)}, u32[]{:S(2)}) collective-permute-start(bf16[512,1024]{1,0:T(8,128)(2,1)} %add.85), channel_id=1, source_target_pairs={{0,24},{8,0},{16,8},{24,16},{1,25},{9,1},{17,9},{25,17},{2,26},{10... | collective-permute-start | bytes 3145736 | tf_op jit(solution)/shard_map/ppermute | solution.py:404
  563.6 49.6 %collective-permute-start.40 = (bf16[512,1024]{1,0:T(8,128)(2,1)}, bf16[512,1024]{1,0:T(8,128)(2,1)}, u32[]{:S(2)}, u32[]{:S(2)}) collective-permute-start(bf16[512,1024]{1,0:T(8,128)(2,1)} %add.84), channel_id=1, source_target_pairs={{0,8},{8,16},{16,24},{24,0},{1,9},{9,17},{17,25},{25,1},{2,10},{10... | collective-permute-start | bytes 3145736 | tf_op jit(solution)/shard_map/ppermute | solution.py:401
  588.7 71.6 %collective-permute-start.13 = (bf16[512,1024]{1,0:T(8,128)(2,1)}, bf16[512,1024]{1,0:T(8,128)(2,1)}, u32[]{:S(2)}, u32[]{:S(2)}) collective-permute-start(bf16[512,1024]{1,0:T(8,128)(2,1)} %get-tuple-element.101), channel_id=1, source_target_pairs={{0,24},{8,0},{16,8},{24,16},{1,25},{9,1},{17,9},{25,17},{2,26},{10... | collective-permute-start | bytes 3145736 | tf_op jit(solution)/shard_map/ppermute | solution.py:404
  592.0 74.4 %collective-permute-start.9 = (bf16[512,1024]{1,0:T(8,128)(2,1)}, bf16[512,1024]{1,0:T(8,128)(2,1)}, u32[]{:S(2)}, u32[]{:S(2)}) collective-permute-start(bf16[512,1024]{1,0:T(8,128)(2,1)} %get-tuple-element.96), channel_id=1, source_target_pairs={{0,8},{8,16},{16,24},{24,0},{1,9},{9,17},{17,25},{25,1},{2,10},{10... | collective-permute-start | bytes 3145736 | tf_op jit(solution)/shard_map/ppermute | solution.py:401
  657.0 48.8 %collective-permute-start.11 = (bf16[512,1024]{1,0:T(8,128)(2,1)}, bf16[512,1024]{1,0:T(8,128)(2,1)}, u32[]{:S(2)}, u32[]{:S(2)}) collective-permute-start(bf16[512,1024]{1,0:T(8,128)(2,1)} %get-tuple-element.97), channel_id=1, source_target_pairs={{0,24},{8,0},{16,8},{24,16},{1,25},{9,1},{17,9},{25,17},{2,26},{10... | collective-permute-start | bytes 3145736 | tf_op jit(solution)/shard_map/ppermute | solution.py:404
  660.3 45.6 %collective-permute-start.12 = (bf16[512,1024]{1,0:T(8,128)(2,1)}, bf16[512,1024]{1,0:T(8,128)(2,1)}, u32[]{:S(2)}, u32[]{:S(2)}) collective-permute-start(bf16[512,1024]{1,0:T(8,128)(2,1)} %get-tuple-element.99), channel_id=1, source_target_pairs={{0,8},{8,16},{16,24},{24,0},{1,9},{9,17},{17,25},{25,1},{2,10},{10... | collective-permute-start | bytes 3145736 | tf_op jit(solution)/shard_map/ppermute | solution.py:401
  663.2 59.6 %collective-permute-start.14 = (bf16[512,1024]{1,0:T(8,128)(2,1)}, bf16[512,1024]{1,0:T(8,128)(2,1)}, u32[]{:S(2)}, u32[]{:S(2)}) collective-permute-start(bf16[512,1024]{1,0:T(8,128)(2,1)} %add.77), channel_id=1, source_target_pairs={{0,24},{8,0},{16,8},{24,16},{1,25},{9,1},{17,9},{25,17},{2,26},{10... | collective-permute-start | bytes 3145736 | tf_op jit(solution)/shard_map/ppermute | solution.py:404
  669.0 54.0 %collective-permute-start.10 = (bf16[512,1024]{1,0:T(8,128)(2,1)}, bf16[512,1024]{1,0:T(8,128)(2,1)S(1)}, u32[]{:S(2)}, u32[]{:S(2)}) collective-permute-start(bf16[512,1024]{1,0:T(8,128)(2,1)} %add.76), channel_id=1, source_target_pairs={{0,8},{8,16},{16,24},{24,0},{1,9},{9,17},{17,25},{25,1},{2,10},{10... | collective-permute-start | bytes 3145736 | tf_op jit(solution)/shard_map/ppermute | solution.py:401
  684.8 77.3 %all-to-all-start.4 = ((bf16[4,512,512]{2,1,0:T(8,128)(2,1)}), bf16[4,512,512]{2,1,0:T(8,128)(2,1)}, u32[]{:S(2)}, u32[]{:S(2)}) async-start(bf16[4,512,512]{2,1,0:T(8,128)(2,1)} %get-tuple-element.134.refs_3_), calls=%async_computation.4 | async-start | bytes 4194304 | tf_op jit(solution)/shard_map/all_to_all | solution.py:515
  762.1 44.5 %all-to-all-start.1 = ((bf16[4,512,512]{2,1,0:T(8,128)(2,1)}), bf16[4,512,512]{2,1,0:T(8,128)(2,1)S(1)}, u32[]{:S(2)}, u32[]{:S(2)}) async-start(bf16[4,512,512]{2,1,0:T(8,128)(2,1)} %get-tuple-element.104.refs_0_), calls=%async_computation.1 | async-start | bytes 4194304 | tf_op jit(solution)/shard_map/all_to_all | solution.py:515
  806.6 85.3 %all-to-all-start.2 = ((bf16[4,512,512]{2,1,0:T(8,128)(2,1)}), bf16[4,512,512]{2,1,0:T(8,128)(2,1)}, u32[]{:S(2)}, u32[]{:S(2)}) async-start(bf16[4,512,512]{2,1,0:T(8,128)(2,1)} %get-tuple-element.105.refs_1_.refs_2_), calls=%async_computation.2 | async-start | bytes 4194304 | tf_op jit(solution)/shard_map/all_to_all | solution.py:515
  843.1 46.7 %collective-permute-start.48 = (bf16[512,1024]{1,0:T(8,128)(2,1)S(1)}, bf16[512,1024]{1,0:T(8,128)(2,1)S(1)}, u32[]{:S(2)}, u32[]{:S(2)}) collective-permute-start(bf16[512,1024]{1,0:T(8,128)(2,1)S(1)} %collective-permute-done.47.refs_6_), channel_id=1, source_target_pairs={{0,2},{2,4},{4,6},{6,0},{1,3},{3,5},{5,7},{7,1},{8,10},{10,12},{12... | collective-permute-start | bytes 3145736 | tf_op jit(solution)/shard_map/ppermute | solution.py:401
  843.1 48.7 %collective-permute-start.49 = (bf16[512,1024]{1,0:T(8,128)(2,1)}, bf16[512,1024]{1,0:T(8,128)(2,1)}, u32[]{:S(2)}, u32[]{:S(2)}) collective-permute-start(bf16[512,1024]{1,0:T(8,128)(2,1)} %collective-permute-done.46.refs_3_), channel_id=1, source_target_pairs={{0,6},{2,0},{4,2},{6,4},{1,7},{3,1},{5,3},{7,5},{8,14},{10,8},{12,... | collective-permute-start | bytes 3145736 | tf_op jit(solution)/shard_map/ppermute | solution.py:404
  846.4 92.5 %collective-permute-start.15 = (bf16[512,1024]{1,0:T(8,128)(2,1)}, bf16[512,1024]{1,0:T(8,128)(2,1)}, u32[]{:S(2)}, u32[]{:S(2)}) collective-permute-start(bf16[512,1024]{1,0:T(8,128)(2,1)} %get-tuple-element.108.refs_0_.refs_6_), channel_id=1, source_target_pairs={{0,6},{2,0},{4,2},{6,4},{1,7},{3,1},{5,3},{7,5},{8,14},{10,8},{12,... | collective-permute-start | bytes 3145736 | tf_op jit(solution)/shard_map/ppermute | solution.py:404
  867.3 71.5 %collective-permute-start.20 = (bf16[512,1024]{1,0:T(8,128)(2,1)}, bf16[512,1024]{1,0:T(8,128)(2,1)}, u32[]{:S(2)}, u32[]{:S(2)}) collective-permute-start(bf16[512,1024]{1,0:T(8,128)(2,1)} %get-tuple-element.109.refs_1_.refs_7_), channel_id=1, source_target_pairs={{0,2},{2,4},{4,6},{6,0},{1,3},{3,5},{5,7},{7,1},{8,10},{10,12},{12... | collective-permute-start | bytes 3145736 | tf_op jit(solution)/shard_map/ppermute | solution.py:401
  867.3 71.5 %collective-permute-start.18 = (bf16[512,1024]{1,0:T(8,128)(2,1)S(1)}, bf16[512,1024]{1,0:T(8,128)(2,1)}, u32[]{:S(2)}, u32[]{:S(2)}) collective-permute-start(bf16[512,1024]{1,0:T(8,128)(2,1)S(1)} %collective-permute-done.17.refs_6_), channel_id=1, source_target_pairs={{0,2},{2,4},{4,6},{6,0},{1,3},{3,5},{5,7},{7,1},{8,10},{10,12},{12... | collective-permute-start | bytes 3145736 | tf_op jit(solution)/shard_map/ppermute | solution.py:401
  890.8 48.1 %collective-permute-start.19 = (bf16[512,1024]{1,0:T(8,128)(2,1)S(1)}, bf16[512,1024]{1,0:T(8,128)(2,1)}, u32[]{:S(2)}, u32[]{:S(2)}) collective-permute-start(bf16[512,1024]{1,0:T(8,128)(2,1)S(1)} %collective-permute-done.16.refs_3_), channel_id=1, source_target_pairs={{0,6},{2,0},{4,2},{6,4},{1,7},{3,1},{5,3},{7,5},{8,14},{10,8},{12,... | collective-permute-start | bytes 3145736 | tf_op jit(solution)/shard_map/ppermute | solution.py:404
  1010.8 77.2 %collective-permute-start.25 = (bf16[512,1024]{1,0:T(8,128)(2,1)}, bf16[512,1024]{1,0:T(8,128)(2,1)}, u32[]{:S(2)}, u32[]{:S(2)}) collective-permute-start(bf16[512,1024]{1,0:T(8,128)(2,1)} %get-tuple-element.117), channel_id=1, source_target_pairs={{0,6},{2,0},{4,2},{6,4},{1,7},{3,1},{5,3},{7,5},{8,14},{10,8},{12,... | collective-permute-start | bytes 3145736 | tf_op jit(solution)/shard_map/ppermute | solution.py:404
  1012.2 78.0 %collective-permute-start.21 = (bf16[512,1024]{1,0:T(8,128)(2,1)}, bf16[512,1024]{1,0:T(8,128)(2,1)}, u32[]{:S(2)}, u32[]{:S(2)}) collective-permute-start(bf16[512,1024]{1,0:T(8,128)(2,1)} %get-tuple-element.112), channel_id=1, source_target_pairs={{0,2},{2,4},{4,6},{6,0},{1,3},{3,5},{5,7},{7,1},{8,10},{10,12},{12... | collective-permute-start | bytes 3145736 | tf_op jit(solution)/shard_map/ppermute | solution.py:401
  1037.9 55.9 %collective-permute-start.55 = (bf16[512,1024]{1,0:T(8,128)(2,1)}, bf16[512,1024]{1,0:T(8,128)(2,1)}, u32[]{:S(2)}, u32[]{:S(2)}) collective-permute-start(bf16[512,1024]{1,0:T(8,128)(2,1)} %get-tuple-element.154), channel_id=1, source_target_pairs={{0,6},{2,0},{4,2},{6,4},{1,7},{3,1},{5,3},{7,5},{8,14},{10,8},{12,... | collective-permute-start | bytes 3145736 | tf_op jit(solution)/shard_map/ppermute | solution.py:404
  1040.4 53.5 %collective-permute-start.51 = (bf16[512,1024]{1,0:T(8,128)(2,1)}, bf16[512,1024]{1,0:T(8,128)(2,1)}, u32[]{:S(2)}, u32[]{:S(2)}) collective-permute-start(bf16[512,1024]{1,0:T(8,128)(2,1)} %get-tuple-element.149), channel_id=1, source_target_pairs={{0,2},{2,4},{4,6},{6,0},{1,3},{3,5},{5,7},{7,1},{8,10},{10,12},{12... | collective-permute-start | bytes 3145736 | tf_op jit(solution)/shard_map/ppermute | solution.py:401
  1040.4 56.7 %collective-permute-start.23 = (bf16[512,1024]{1,0:T(8,128)(2,1)}, bf16[512,1024]{1,0:T(8,128)(2,1)S(1)}, u32[]{:S(2)}, u32[]{:S(2)}) collective-permute-start(bf16[512,1024]{1,0:T(8,128)(2,1)} %get-tuple-element.113), channel_id=1, source_target_pairs={{0,6},{2,0},{4,2},{6,4},{1,7},{3,1},{5,3},{7,5},{8,14},{10,8},{12,... | collective-permute-start | bytes 3145736 | tf_op jit(solution)/shard_map/ppermute | solution.py:404
  1088.0 62.1 %collective-permute-start.53 = (bf16[512,1024]{1,0:T(8,128)(2,1)}, bf16[512,1024]{1,0:T(8,128)(2,1)S(1)}, u32[]{:S(2)}, u32[]{:S(2)}) collective-permute-start(bf16[512,1024]{1,0:T(8,128)(2,1)} %get-tuple-element.150), channel_id=1, source_target_pairs={{0,6},{2,0},{4,2},{6,4},{1,7},{3,1},{5,3},{7,5},{8,14},{10,8},{12,... | collective-permute-start | bytes 3145736 | tf_op jit(solution)/shard_map/ppermute | solution.py:404
  1090.2 59.9 %collective-permute-start.54 = (bf16[512,1024]{1,0:T(8,128)(2,1)}, bf16[512,1024]{1,0:T(8,128)(2,1)}, u32[]{:S(2)}, u32[]{:S(2)}) collective-permute-start(bf16[512,1024]{1,0:T(8,128)(2,1)} %get-tuple-element.152), channel_id=1, source_target_pairs={{0,2},{2,4},{4,6},{6,0},{1,3},{3,5},{5,7},{7,1},{8,10},{10,12},{12... | collective-permute-start | bytes 3145736 | tf_op jit(solution)/shard_map/ppermute | solution.py:401
  1146.9 51.8 %collective-permute-start.27 = (bf16[512,1024]{1,0:T(8,128)(2,1)}, bf16[512,1024]{1,0:T(8,128)(2,1)}, u32[]{:S(2)}, u32[]{:S(2)}) collective-permute-start(bf16[512,1024]{1,0:T(8,128)(2,1)} %get-tuple-element.118), channel_id=1, source_target_pairs={{0,24},{8,0},{16,8},{24,16},{1,25},{9,1},{17,9},{25,17},{2,26},{10... | collective-permute-start | bytes 3145736 | tf_op jit(solution)/shard_map/ppermute | solution.py:404
  1150.1 44.8 %collective-permute-start.28 = (bf16[512,1024]{1,0:T(8,128)(2,1)}, bf16[512,1024]{1,0:T(8,128)(2,1)}, u32[]{:S(2)}, u32[]{:S(2)}) collective-permute-start(bf16[512,1024]{1,0:T(8,128)(2,1)} %get-tuple-element.119), channel_id=1, source_target_pairs={{0,24},{8,0},{16,8},{24,16},{1,25},{9,1},{17,9},{25,17},{2,26},{10... | collective-permute-start | bytes 3145736 | tf_op jit(solution)/shard_map/ppermute | solution.py:404
  1168.4 51.9 %collective-permute-start.58 = (bf16[512,1024]{1,0:T(8,128)(2,1)}, bf16[512,1024]{1,0:T(8,128)(2,1)S(1)}, u32[]{:S(2)}, u32[]{:S(2)}) collective-permute-start(bf16[512,1024]{1,0:T(8,128)(2,1)} %get-tuple-element.156), channel_id=1, source_target_pairs={{0,24},{8,0},{16,8},{24,16},{1,25},{9,1},{17,9},{25,17},{2,26},{10... | collective-permute-start | bytes 3145736 | tf_op jit(solution)/shard_map/ppermute | solution.py:404
  1168.5 54.0 %collective-permute-start.59 = (bf16[512,1024]{1,0:T(8,128)(2,1)}, bf16[512,1024]{1,0:T(8,128)(2,1)S(1)}, u32[]{:S(2)}, u32[]{:S(2)}) collective-permute-start(bf16[512,1024]{1,0:T(8,128)(2,1)} %get-tuple-element.155), channel_id=1, source_target_pairs={{0,8},{8,16},{16,24},{24,0},{1,9},{9,17},{17,25},{25,1},{2,10},{10... | collective-permute-start | bytes 3145736 | tf_op jit(solution)/shard_map/ppermute | solution.py:401
  (67 other events, 1710.5 us)
Sparse Core Ops, SparseCore 0:
  11.6 71.6 all-gather.8
  85.4 45.3 all-gather.10
  132.4 81.9 all-gather.12
  215.8 47.6 all-gather.14
  265.5 155.8 all-gather.16
  422.8 167.0 all-gather.18
where the time goes:
time: 1280 us; the launch traced here: 1270 us
  Pallas kernels  585 us (46%)
  waiting for transfers between devices  334 us (26%)
  starting transfers between devices  101 us (8%)
  blocking collectives  92.2 us (7%)
  local copies, waits for them, and re-layouts  79.4 us (6%)
  other arithmetic  53.2 us (4%)
  between operations  22.6 us (2%)
    ppermute x31, waiting for transfers between devices, up(): lax.ppermute(a, self.axis, [(i, (i + 1) % self.size) for i in range(self....  218 us
    pallas_call x8, Pallas kernels, mlp_up(): pl.pallas_call(body, grid=(steps,), in_specs=[fixed] * (2 * seqs) + [gate...  189 us
    pallas_call x4, Pallas kernels, mlp_down(): pl.pallas_call(body, grid=(2 * per_side,), in_specs=[pl.BlockSpec(a.shape...  100 us
    ppermute x31, waiting for transfers between devices, down(): lax.ppermute(a, self.axis, [(i, (i - 1) % self.size) for i in range(self....  95.9 us
    pallas_call x4, Pallas kernels, attention(): pl.pallas_call(body, grid=(seqs,), in_specs=[pl.BlockSpec((1, qc, group),...  75.8 us
    ppermute x31, starting transfers between devices, down(): lax.ppermute(a, self.axis, [(i, (i - 1) % self.size) for i in range(self....  66 us
    pallas_call x2, Pallas kernels, qkv_full(): pl.pallas_call(body, grid=(3, blocks), in_specs=[fixed((tokens, width)),...  65.4 us
    pallas_call x2, Pallas kernels, out_proj_gathered(): pl.pallas_call(body, grid_spec=pltpu.PrefetchScalarGridSpec(num_scalar_pr...  60.8 us
  transfers between devices with their start and end apart: 73, of which 25 were waited for; matrix products, arithmetic and copies ran while one was open for 9% of the time, Pallas kernels for 41%

commit v1 on v0

--- a/solution.py
+++ b/solution.py
@@ -148,67 +148,108 @@
     seqs, qc, half = outs[0].shape
     width = x.shape[2]
     shards, sources, _, cols = w.shape
+    depth = 2 * half
+    group = 2
+    rows = group * qc
 
     def body(order_ref, *refs):
-        o_refs, (w_ref, x_ref, gain_ref, ha_ref, hb_ref, a_ref) = refs[:2 * sources], refs[2 * sources:]
-        sq = jnp.zeros((qc, 1), F32)
+        o_refs, (w_ref, x0_ref, x1_ref, gain_ref, ha_ref, hb_ref, o_ref, a_ref, sems) = refs[:2 * sources], refs[2 * sources:]
+        step = pl.program_id(0)
+
+        def copies(g):
+            for j in range(group):
+                for s in range(sources):
+                    for side in range(2):
+                        at = pl.multiple_of(order_ref[s] * depth + side * half, half)
+                        yield pltpu.make_async_copy(
+                            o_refs[2 * s + side].at[order_ref[g * group + j]],
+                            o_ref.at[g, pl.ds(j * qc, qc), pl.ds(at, half)], sems.at[g])
+
+        @pl.when(step == 0)
+        def _():
+            for g in range(seqs // group):
+                for c in copies(g):
+                    c.start()
+
+        for c in copies(step):
+            c.wait()
+        sq = jnp.zeros((rows, 1), F32)
         for f in range(shards):
-            acc = jnp.zeros((qc, cols), F32)
-            for s in range(sources):
-                src = order_ref[s]
-                acc += dot(o_refs[2 * s][0], w_ref[f, src, :half, :])
-                acc += dot(o_refs[2 * s + 1][0], w_ref[f, src, half:, :])
-            a = acc.astype(BF16)
+            a = dot(o_ref[step], w_ref[f].reshape(width, cols)).astype(BF16)
             a_ref[:, f * cols:(f + 1) * cols] = a
             a = a.astype(F32)
             sq += jnp.sum(a * a, axis=-1, keepdims=True)
         inv = lax.rsqrt(sq / width + NORM_EPS)
-        for f in range(shards):
-            c = slice(f * cols, (f + 1) * cols)
-            h_ref = (ha_ref, hb_ref)[f // (shards // 2)]
-            hc = slice(f % (shards // 2) * cols, (f % (shards // 2) + 1) * cols)
-            h_ref[0, :, hc] = (x_ref[0, :, c].astype(F32) + a_ref[:, c].astype(F32) * inv * gain_ref[:, c]).astype(BF16)
-
-    o_spec = pl.BlockSpec((1, qc, half), lambda r, order: (order[r], 0, 0))
+        for j, x_ref in enumerate((x0_ref, x1_ref)):
+            r = slice(j * qc, (j + 1) * qc)
+            for f in range(shards):
+                c = slice(f * cols, (f + 1) * cols)
+                h_ref = (ha_ref, hb_ref)[f // (shards // 2)]
+                hc = slice(f % (shards // 2) * cols, (f % (shards // 2) + 1) * cols)
+                h_ref[j, :, hc] = (x_ref[0, :, c].astype(F32) + a_ref[r, c].astype(F32) * inv[r] * gain_ref[:, c]).astype(BF16)
+
+    x_spec = lambda j: pl.BlockSpec((1, qc, width), lambda g, order: (order[g * group + j], chunk, 0))
     return pl.pallas_call(
         body,
         grid_spec=pltpu.PrefetchScalarGridSpec(
-            num_scalar_prefetch=1, grid=(seqs,),
-            in_specs=[o_spec] * (2 * sources) + [
-                pl.BlockSpec(w.shape, lambda r, order: (0, 0, 0, 0), pipeline_mode=pl.Buffered(1)),
-                pl.BlockSpec((1, qc, width), lambda r, order: (order[r], chunk, 0)),
-                pl.BlockSpec((1, width), lambda r, order: (0, 0))],
-            out_specs=[pl.BlockSpec((1, qc, width // 2), lambda r, order: (r, 0, 0))] * 2,
-            scratch_shapes=[pltpu.VMEM((qc, width), BF16)]),
+            num_scalar_prefetch=1, grid=(seqs // group,),
+            in_specs=[pl.BlockSpec(memory_space=pl.ANY)] * (2 * sources) + [
+                pl.BlockSpec(w.shape, lambda g, order: (0, 0, 0, 0), pipeline_mode=pl.Buffered(1)), x_spec(0), x_spec(1),
+                pl.BlockSpec((1, width), lambda g, order: (0, 0))],
+            out_specs=[pl.BlockSpec((group, qc, width // 2), lambda g, order: (g, 0, 0))] * 2,
+            scratch_shapes=[pltpu.VMEM((seqs // group, rows, width), BF16), pltpu.VMEM((rows, width), BF16),
+                            pltpu.SemaphoreType.DMA((seqs // group,))]),
         out_shape=[jax.ShapeDtypeStruct((seqs, qc, width // 2), BF16)] * 2,
-        compiler_params=params(), cost_estimate=cost(2 * seqs * qc * width * width, 6 * seqs * qc * width + 2 * width * width))(order, *outs, w, x, gain)
+        compiler_params=params(), cost_estimate=cost(2 * seqs * qc * width * width, 6 * seqs * qc * width + 2 * width * width))(order, *outs, w, x, x, gain)
 
 
 def mlp_up(hs, w, gate_spec, up_spec, first, steps):
     seqs = len(hs)
-    qc, half = hs[0][0].shape
+    qc, half = hs[0][0].shape[-2:]
     width = 2 * half
     tn = 256
+    group = 2
+    rows = seqs * qc
 
     def body(*refs):
-        h_refs, (g_ref, u_ref, act_ref) = refs[:2 * seqs], refs[2 * seqs:]
+        h_refs, (g_ref, u_ref, act_ref, h_ref, sems) = refs[:2 * seqs], refs[2 * seqs:]
+        step = pl.program_id(0)
+
+        def copies(p):
+            for q in range(group):
+                n = p * group + q
+                for side in range(2):
+                    src = h_refs[2 * n + side]
+                    src = src if hs[n][2] is None else src.at[hs[n][2]]
+                    yield pltpu.make_async_copy(src, h_ref.at[pl.ds(n * qc, qc), pl.ds(side * half, half)], sems.at[p])
+
+        @pl.when(step == 0)
+        def _():
+            for p in range(seqs // group):
+                for c in copies(p):
+                    c.start()
+
         g = g_ref[...].reshape(width, tn)
         u = u_ref[...].reshape(width, tn)
-        for s in range(seqs):
-            ha, hb = h_refs[2 * s][...], h_refs[2 * s + 1][...]
-            gate = dot(ha, g[:half]) + dot(hb, g[half:])
-            up = dot(ha, u[:half]) + dot(hb, u[half:])
-            act_ref[s * qc:(s + 1) * qc, :] = (jax.nn.silu(gate) * up).astype(BF16)
+        for p in range(seqs // group):
+            @pl.when(step == 0)
+            def _(p=p):
+                for c in copies(p):
+                    c.wait()
+
+            r = slice(p * group * qc, (p + 1) * group * qc)
+            gate = dot(h_ref[r, :], g)
+            up = dot(h_ref[r, :], u)
+            act_ref[r, :] = (jax.nn.silu(gate) * up).astype(BF16)
 
     index = lambda i: first + i
-    fixed = pl.BlockSpec((qc, half), lambda i: (0, 0), pipeline_mode=pl.Buffered(1))
-    rows = seqs * qc
-    flat = [a for pair in hs for a in pair]
+    flat = [a for pair in hs for a in pair[:2]]
     return pl.pallas_call(
         body, grid=(steps,),
-        in_specs=[fixed] * (2 * seqs) + [gate_spec(index), up_spec(index)],
+        in_specs=[pl.BlockSpec(memory_space=pl.ANY)] * (2 * seqs) + [gate_spec(index), up_spec(index)],
         out_specs=pl.BlockSpec((rows, tn), lambda i: (0, i)),
         out_shape=jax.ShapeDtypeStruct((rows, steps * tn), BF16),
+        scratch_shapes=[pltpu.VMEM((rows, width), BF16), pltpu.SemaphoreType.DMA((seqs // group,))],
         compiler_params=params(), cost_estimate=cost(4 * rows * width * steps * tn, 2 * rows * width + 4 * width * steps * tn))(*flat, w, w)
 
 
@@ -220,42 +261,56 @@
     tn = 256
     half = width // 2
     per_side = half // tn
+    group = 2
 
     def body(*refs):
-        act_refs, d_ref, outs = refs[:n], refs[n], refs[n + 1:]
+        act_refs, d_ref, outs, act_ref, sems = refs[:n], refs[n], refs[n + 1:-2], refs[-2], refs[-1]
+        step = pl.program_id(0)
+
+        def copies(p):
+            at = 0
+            r = pl.ds(p * group * qc, group * qc)
+            for a, ref in zip(acts, act_refs):
+                yield pltpu.make_async_copy(ref.at[r, :], act_ref.at[r, pl.ds(at, a.shape[1])], sems.at[p])
+                at += a.shape[1]
+
+        @pl.when(step == 0)
+        def _():
+            for p in range(seqs // group):
+                for c in copies(p):
+                    c.start()
+
         d = d_ref[...].reshape(ff, tn)
-        step = pl.program_id(0)
-
-        def product(s):
-            acc = jnp.zeros((qc, tn), F32)
-            at = 0
-            for a in act_refs:
-                acc += dot(a[s * qc:(s + 1) * qc, :], d[at:at + a.shape[1]])
-                at += a.shape[1]
-            return acc.astype(BF16)
-
-        for side in range(2):
-            @pl.when(step // per_side == side)
-            def _(side=side):
-                for s in range(seqs):
-                    outs[2 * s + side][...] = product(s)
+        for p in range(seqs // group):
+            @pl.when(step == 0)
+            def _(p=p):
+                for c in copies(p):
+                    c.wait()
+
+            m = dot(act_ref[p * group * qc:(p + 1) * group * qc, :], d).astype(BF16)
+            for side in range(2):
+                @pl.when(step // per_side == side)
+                def _(side=side, m=m, p=p):
+                    for q in range(group):
+                        outs[2 * (p * group + q) + side][...] = m[q * qc:(q + 1) * qc]
 
     first = pl.BlockSpec((qc, tn), lambda i: (0, jnp.minimum(i, per_side - 1)))
     second = pl.BlockSpec((qc, tn), lambda i: (0, jnp.maximum(i - per_side, 0)))
     return pl.pallas_call(
         body, grid=(2 * per_side,),
-        in_specs=[pl.BlockSpec(a.shape, lambda i: (0, 0), pipeline_mode=pl.Buffered(1)) for a in acts] + [down_spec(lambda i: i)],
+        in_specs=[pl.BlockSpec(memory_space=pl.ANY)] * n + [down_spec(lambda i: i)],
         out_specs=[first, second] * seqs,
         out_shape=[jax.ShapeDtypeStruct((qc, half), BF16)] * (2 * seqs),
+        scratch_shapes=[pltpu.VMEM((rows, ff), BF16), pltpu.SemaphoreType.DMA((seqs // group,))],
         compiler_params=params(), cost_estimate=cost(2 * rows * width * ff, 2 * rows * (width + ff) + 2 * width * ff))(*acts, w)
 
 
 def finish(parts_a, parts_b, h_a, h_b, gain, place, whole):
-    rows, half = h_a.shape
+    rows, half = h_a.shape[-2:]
     width = 2 * half
     block = 256
     per_side = half // block
-    tr = min(256, rows)
+    tr = min(128, rows)
     n = len(parts_a)
 
     def body(*refs):
@@ -274,7 +329,7 @@
                 c = slice(b * block, (b + 1) * block)
                 at = place(side, b)
                 gain_cols = gain_ref[:, at * block:(at + 1) * block]
-                val = (h_refs[side][:, c].astype(F32) + sums[side][:, c] * inv * gain_cols).astype(BF16)
+                val = (h_refs[side][0, :, c].astype(F32) + sums[side][:, c] * inv * gain_cols).astype(BF16)
                 if whole:
                     outs[0][:, at * block:(at + 1) * block] = val
                 else:
@@ -286,10 +341,11 @@
     outs = 1 if whole else 2
     return pl.pallas_call(
         body, grid=(rows // tr,),
-        in_specs=[part] * (2 * n + 2) + [pl.BlockSpec((1, width), lambda i: (0, 0))],
+        in_specs=[part] * (2 * n) + [pl.BlockSpec((1, tr, half), lambda i: (0, i, 0))] * 2
+        + [pl.BlockSpec((1, width), lambda i: (0, 0))],
         out_specs=[pl.BlockSpec((tr, out_width), lambda i: (i, 0))] * outs,
         out_shape=[jax.ShapeDtypeStruct((rows, out_width), BF16)] * outs,
-        compiler_params=params(), cost_estimate=cost(rows * width * 2000, rows * width * 2 * (n + 2)))(*parts_a, *parts_b, h_a, h_b, gain)
+        compiler_params=params(), cost_estimate=cost(rows * width * 2000, rows * width * 2 * (n + 2)))(*parts_a, *parts_b, *(h if h.ndim == 3 else h[None] for h in (h_a, h_b)), gain)
 
 
 def qkv_full(x, w, q_gain, k_gain, cos_t, sin_t, part, chunk):
@@ -297,51 +353,53 @@
     shards, tps, _, cols = w.shape
     depth = width // shards
     per = part // cols
-    blocks = tps * per
-    tr = min(256, tokens)
-
-    def body(x_ref, w_ref, qg_ref, kg_ref, cos_ref, sin_ref, q_ref, k_ref, v_ref, raw_ref, sq_ref):
-        which, n = pl.program_id(0), pl.program_id(1)
-        out = dot(x_ref[...], w_ref[...].reshape(width, cols))
-
-        @pl.when(which < 2)
-        def _():
-            raw_ref[n] = out
-            part_sq = jnp.sum(out * out, axis=-1, keepdims=True)
-            sq_ref[...] = jnp.where(n == 0, 0.0, sq_ref[...]) + part_sq
+
+    def body(x_ref, w_ref, qg_ref, kg_ref, cos_ref, sin_ref, q_ref, k_ref, v_ref, q_raw, k_raw, q_sq, k_sq):
+        which, t = pl.program_id(0), pl.program_id(1)
+
+        def product(b):
+            return dot(x_ref[...], w_ref[:, 0, b * depth:(b + 1) * depth, :].reshape(width, cols))
+
+        def keep(raw, sq):
+            total = jnp.where(t == 0, 0.0, sq[...])
+            for b in range(per):
+                out = product(b)
+                raw[t, :, b * cols:(b + 1) * cols] = out
+                total += jnp.sum(out * out, axis=-1, keepdims=True)
+            sq[...] = total
+
+        def rotated(raw, sq, gain_ref, dst):
+            inv = lax.rsqrt(sq[...] / width + NORM_EPS)
+            for h in range(part // HEAD_DIM):
+                c = slice(h * HEAD_DIM, (h + 1) * HEAD_DIM)
+                vals = raw[t, :, c] * inv * gain_ref[:, c]
+                dst[0, :, c] = rotate(vals, cos_ref[...], sin_ref[...]).astype(BF16)
+
+        @pl.when(which == 0)
+        def _():
+            keep(q_raw, q_sq)
+
+        @pl.when(which == 1)
+        def _():
+            keep(k_raw, k_sq)
+            rotated(q_raw, q_sq, qg_ref, q_ref)
 
         @pl.when(which == 2)
         def _():
-            v_ref[0] = out.astype(BF16)
-
-        for sel, (gain, dst) in enumerate(((qg_ref, q_ref), (kg_ref, k_ref))):
-            @pl.when((which == sel) & (n == blocks - 1))
-            def _(gain=gain, dst=dst):
-                def rows_body(r, _):
-                    rows = pl.ds(r * tr, tr)
-                    inv = lax.rsqrt(sq_ref[rows, :] / width + NORM_EPS)
-                    for m in range(blocks):
-                        for h in range(cols // HEAD_DIM):
-                            lanes = slice(h * HEAD_DIM, (h + 1) * HEAD_DIM)
-                            wide = slice(m * cols + h * HEAD_DIM, m * cols + (h + 1) * HEAD_DIM)
-                            deep = slice(m % per * cols + h * HEAD_DIM, m % per * cols + (h + 1) * HEAD_DIM)
-                            vals = raw_ref[m, rows, lanes] * inv * gain[:, wide]
-                            dst[m // per, rows, deep] = rotate(vals, cos_ref[rows, :], sin_ref[rows, :]).astype(BF16)
-                    return 0
-
-                lax.fori_loop(0, tokens // tr, rows_body, 0)
-
-    fixed = lambda s: pl.BlockSpec(s, lambda i, n: (0,) * len(s), pipeline_mode=pl.Buffered(1))
-    whole = pl.BlockSpec((tps, tokens, part), lambda i, n: (0, 0, 0))
-    table = pl.BlockSpec((tokens, HEAD_DIM), lambda i, n: (chunk, 0), pipeline_mode=pl.Buffered(1))
-    return pl.pallas_call(
-        body, grid=(3, blocks),
-        in_specs=[fixed((tokens, width)),
-                  pl.BlockSpec((shards, 1, depth, cols), lambda i, n: (0, n // per, i * per + n % per, 0)),
-                  fixed((1, width)), fixed((1, width)), table, table],
-        out_specs=[whole, whole, pl.BlockSpec((1, tokens, cols), lambda i, n: (jnp.where(i == 2, n // per, 0), 0, jnp.where(i == 2, n % per, 0)))],
+            for b in range(per):
+                v_ref[0, :, b * cols:(b + 1) * cols] = product(b).astype(BF16)
+            rotated(k_raw, k_sq, kg_ref, k_ref)
+
+    table = pl.BlockSpec((tokens, HEAD_DIM), lambda i, t: (chunk, 0), pipeline_mode=pl.Buffered(1))
+    gain = pl.BlockSpec((1, part), lambda i, t: (0, t))
+    late = pl.BlockSpec((1, tokens, part), lambda i, t: (jnp.where(i == 2, t, 0), 0, 0))
+    return pl.pallas_call(
+        body, grid=(3, tps),
+        in_specs=[pl.BlockSpec((tokens, width), lambda i, t: (0, 0), pipeline_mode=pl.Buffered(1)),
+                  pl.BlockSpec((shards, 1, per * depth, cols), lambda i, t: (0, t, i, 0)), gain, gain, table, table],
+        out_specs=[pl.BlockSpec((1, tokens, part), lambda i, t: (jnp.where(i == 1, t, jnp.where(i == 0, 0, tps - 1)), 0, 0)), late, late],
         out_shape=[jax.ShapeDtypeStruct((tps, tokens, part), BF16)] * 3,
-        scratch_shapes=[pltpu.VMEM((blocks, tokens, cols), F32), pltpu.VMEM((tokens, 1), F32)],
+        scratch_shapes=[pltpu.VMEM((tps, tokens, part), F32)] * 2 + [pltpu.VMEM((tokens, 1), F32)] * 2,
         compiler_params=params("arbitrary", "arbitrary"),
         cost_estimate=cost(6 * tokens * width * width, 8 * tokens * width + 6 * width * width))(x, w, q_gain, k_gain, cos_t, sin_t)
 
@@ -350,6 +408,7 @@
     tokens, width = x.shape
     shards, tps, _, cols = w.shape
     half = depth // 2
+    group = 2
     tr = min(256, tokens)
 
     def body(oa_ref, ob_ref, w_ref, x_ref, gain_ref, ha_ref, hb_ref, o_ref, raw_ref, sq_ref):
@@ -361,12 +420,15 @@
                 o_ref[:, t * depth:t * depth + half] = oa_ref[t]
                 o_ref[:, t * depth + half:(t + 1) * depth] = ob_ref[t]
 
-        out = dot(o_ref[...], w_ref[...].reshape(tps * depth, cols)).astype(BF16)
-        raw_ref[f] = out
-        out = out.astype(F32)
-        sq_ref[...] = jnp.where(f == 0, 0.0, sq_ref[...]) + jnp.sum(out * out, axis=-1, keepdims=True)
-
-        @pl.when(f == shards - 1)
+        total = jnp.where(f == 0, 0.0, sq_ref[...])
+        for b in range(group):
+            out = dot(o_ref[...], w_ref[b].reshape(tps * depth, cols)).astype(BF16)
+            raw_ref[f * group + b] = out
+            out = out.astype(F32)
+            total += jnp.sum(out * out, axis=-1, keepdims=True)
+        sq_ref[...] = total
+
+        @pl.when(f == shards // group - 1)
         def _():
             def rows_body(r, _):
                 rows = pl.ds(r * tr, tr)
@@ -382,8 +444,8 @@
 
     fixed = lambda s: pl.BlockSpec(s, lambda f: (0,) * len(s), pipeline_mode=pl.Buffered(1))
     return pl.pallas_call(
-        body, grid=(shards,),
-        in_specs=[fixed(o_a.shape), fixed(o_b.shape), pl.BlockSpec((1, tps, depth, cols), lambda f: (f, 0, row_block, 0)),
+        body, grid=(shards // group,),
+        in_specs=[fixed(o_a.shape), fixed(o_b.shape), pl.BlockSpec((group, tps, depth, cols), lambda f: (f, 0, row_block, 0)),
                   fixed((tokens, width)), fixed((1, width))],
         out_specs=[pl.BlockSpec((tokens, width // 2), lambda f: (0, 0))] * 2,
         out_shape=[jax.ShapeDtypeStruct((tokens, width // 2), BF16)] * 2,
@@ -402,6 +464,27 @@
 
     def down(self, a):
         return lax.ppermute(a, self.axis, [(i, (i - 1) % self.size) for i in range(self.size)])
+
+    def far(self, a):
+        return lax.ppermute(a, self.axis, [(i, (i + 2) % self.size) for i in range(self.size)])
+
+    def collect(self, a):
+        me = lax.axis_index(self.axis)
+        out = jnp.zeros((self.size, *a.shape), a.dtype)
+        pieces = [(0, a), (1, self.down(a)), (3, self.up(a)), (2, self.far(a))]
+        for rel, piece in pieces:
+            out = lax.dynamic_update_index_in_dim(out, piece, lax.rem(me + rel, self.size), 0)
+        return out
+
+    def exchange(self, pieces):
+        me = lax.axis_index(self.axis)
+        piece = lambda rel: lax.dynamic_index_in_dim(pieces, lax.rem(me + rel, self.size), 0, keepdims=False)
+        got = [(0, piece(0)), (3, self.up(piece(1))), (1, self.down(piece(3))),
+               (2, self.far(piece(2)))]
+        out = jnp.zeros(pieces.shape, pieces.dtype)
+        for rel, a in got:
+            out = lax.dynamic_update_index_in_dim(out, a, lax.rem(me + rel, self.size), 0)
+        return out
 
     def gather(self, a, b):
         below_a, above_b = self.up(a), self.down(b)
@@ -455,18 +538,20 @@
 
         w_qkv = lax.all_gather(jnp.concatenate([w_query[0], w_key[0], w_value[0]], axis=1), shards, axis=0, tiled=True)
         fsdp_gains = lax.all_gather(jnp.stack([attn_norm_w, ffn_norm_w]), shards, axis=2, tiled=True)
-        tp_gains = lax.all_gather(jnp.stack([q_norm_w[1], k_norm_w[1]]), 'tp', axis=1, tiled=True)
-        x, fsdp_gains, tp_gains = lax.optimization_barrier((x, fsdp_gains, tp_gains))
+        tp_gains = ring_y.collect(jnp.stack([q_norm_w[1], k_norm_w[1]]))
+        q_gain1, k_gain1 = tp_gains[:, 0].reshape(1, width), tp_gains[:, 1].reshape(1, width)
+        x, fsdp_gains, q_gain1, k_gain1 = lax.optimization_barrier((x, fsdp_gains, q_gain1, k_gain1))
         w_o0 = gather_all(w_out[0])
         w_gu0 = lax.all_gather(jnp.concatenate([w_gate[0], w_up[0]], axis=1), shards, axis=0, tiled=True)
         w_d0 = lax.all_gather(w_down[0], shards, axis=0, tiled=False)
-        w_attn1 = gather_all(jnp.concatenate(
-            blocks_of(w_query[1], cols) + blocks_of(w_key[1], cols) + blocks_of(w_value[1], cols) + [w_out[1]], axis=0))
+        w_attn1 = jnp.concatenate(
+            blocks_of(w_query[1], cols) + blocks_of(w_key[1], cols) + blocks_of(w_value[1], cols) + [w_out[1]], axis=0)
+        w_attn1 = lax.all_gather(ring_y.collect(w_attn1), shards, axis=0, tiled=False)
         share = ff // xs
         pieces = [jnp.concatenate(blocks_of(w_gate[1][:, i * share:(i + 1) * share], cols)
                                   + blocks_of(w_up[1][:, i * share:(i + 1) * share], cols)
                                   + [w_down[1][i * share:(i + 1) * share]], axis=0) for i in range(xs)]
-        mlp1 = lax.all_to_all(jnp.stack(pieces), 'x', split_axis=0, concat_axis=0, tiled=True)
+        mlp1 = ring_x.exchange(jnp.stack(pieces))
         mlp1 = lax.all_gather(mlp1, ('c', 'tp'), axis=0, tiled=False)
         mlp1 = mlp1.reshape(cores, tp, *mlp1.shape[1:])
         depth = w_gate.shape[1]
@@ -498,8 +583,8 @@
         for c in range(CHUNKS):
             outs = [a for pair in gathered[c] for a in pair]
             h_a, h_b = out_proj_gathered(seq_order, outs, w_o0, x, fsdp_gains[0, :1], c)
-            sums.append(mlp([(h_a[s], h_b[s]) for s in range(batch)], w_gu0, gate0, up0, w_d0, down0, ff))
-            own_h.append((h_a[0], h_b[0]))
+            sums.append(mlp([(h_a, h_b, s) for s in range(batch)], w_gu0, gate0, up0, w_d0, down0, ff))
+            own_h.append((h_a, h_b))
 
         def up_spec(block):
             return lambda index: pl.BlockSpec((cores, 1, xs, depth, 256),
@@ -511,7 +596,7 @@
         for c in range(CHUNKS):
             sum_a, sum_b = ring_y.scatter(sums[c])
             hidden, = finish(sum_a, sum_b, *own_h[c], fsdp_gains[1, :1], lambda side, b: side * per_side + b, True)
-            q1, k1, v1 = qkv_full(hidden, w_attn1, tp_gains[:1], tp_gains[1:], cos_t, sin_t, part, c)
+            q1, k1, v1 = qkv_full(hidden, w_attn1, q_gain1, k_gain1, cos_t, sin_t, part, c)
             caches.append([lax.all_to_all(a, 'tp', split_axis=0, concat_axis=0, tiled=True) for a in (k1, v1)])
             kvs.append((k1, v1, qc))
             own = attention(q1, 0, qc, list(kvs))
@@ -523,7 +608,11 @@
             hs = gathered[c]
             if c == CHUNKS - 1:
                 hs, caches = lax.optimization_barrier((hs, caches))
-            sums.append(mlp(hs, mlp1, gate1, up1, mlp1, down1, tp * share))
+            sums.append(mlp([(*pair, None) for pair in hs], mlp1, gate1, up1, mlp1, down1, tp * share))
+        layers5 = lambda a: a.reshape(1, batch, seq_len, part // HEAD_DIM, HEAD_DIM)
+        caches = [jnp.concatenate([caches[c][n] for c in range(CHUNKS)], axis=1) for n in range(2)]
+        first = lax.optimization_barrier((keys_rot, values, sums[-1][0]))[:2]
+        first = lax.optimization_barrier([layers5(a) for a in first])
         y = jnp.zeros(x.shape, BF16)
         for c in range(CHUNKS):
             sum_a, sum_b = ring_x.scatter(sums[c])
@@ -532,11 +621,12 @@
                 for side in range(2):
                     y = lax.dynamic_update_slice(y, pair[side][None], (seq_order[rel], c * qc, side * width // 2))
 
-        def cache(first, n):
-            second = jnp.concatenate([caches[c][n] for c in range(CHUNKS)], axis=1)
-            return jnp.stack([first, second]).reshape(2, batch, seq_len, part // HEAD_DIM, HEAD_DIM)
-
-        return y, cache(keys_rot, 0), cache(values, 1)
+            if c < CHUNKS - 1:
+                second = lax.optimization_barrier((*caches, y_own[0]))[:2]
+                second = lax.optimization_barrier([layers5(a) for a in second])
+            else:
+                first = lax.optimization_barrier((*first, y_own[0]))[:2]
+        return y, *(jnp.concatenate([a, b], axis=0) for a, b in zip(first, second))
 
     return jax.shard_map(local_layers, mesh=mesh,
                          in_specs=(act_spec, in_cols, in_cols, in_cols, in_rows, in_cols, in_cols, in_rows,

time: 1280 us -> 1330 us (1.039)
  the two profiles are of different devices: /device:TPU:96 before, /device:TPU:100 now
where the time goes in v1:
time: 1330 us; the launch traced here: 1320 us
  Pallas kernels  646 us (49%)
  waiting for transfers between devices  368 us (28%)
  starting transfers between devices  126 us (9%)
  local copies, waits for them, and re-layouts  84.8 us (6%)
  other arithmetic  48.1 us (4%)
  between operations  22.8 us (2%)
  blocking collectives  21.7 us (2%)
    ppermute x34, waiting for transfers between devices, down(): lax.ppermute(a, self.axis, [(i, (i - 1) % self.size) for i in range(self....  208 us
    pallas_call x8, Pallas kernels, mlp_up(): pl.pallas_call(body, grid=(steps,), in_specs=[pl.BlockSpec(memory_space=p...  196 us
    pallas_call x4, Pallas kernels, mlp_down(): pl.pallas_call(body, grid=(2 * per_side,), in_specs=[pl.BlockSpec(memory_...  175 us
    ppermute x34, waiting for transfers between devices, up(): lax.ppermute(a, self.axis, [(i, (i + 1) % self.size) for i in range(self....  141 us
    pallas_call x4, Pallas kernels, attention(): pl.pallas_call(body, grid=(seqs,), in_specs=[pl.BlockSpec((1, qc, group),...  75.8 us
    ppermute x34, starting transfers between devices, down(): lax.ppermute(a, self.axis, [(i, (i - 1) % self.size) for i in range(self....  65.4 us
    pallas_call x2, Pallas kernels, out_proj_gathered(): pl.pallas_call(body, grid_spec=pltpu.PrefetchScalarGridSpec(num_scalar_pr...  63.9 us
    pallas_call x2, Pallas kernels, qkv_full(): pl.pallas_call(body, grid=(3, tps), in_specs=[pl.BlockSpec((tokens, width...  44 us
  transfers between devices with their start and end apart: 82, of which 27 were waited for; matrix products, arithmetic and copies ran while one was open for 8% of the time, Pallas kernels for 42%

profile of v1, /device:TPU:100, one launch (start us, length us, event | category | flops | bytes accessed | tf_op | source)
XLA Modules:
  0.0 1317.7 jit_solution(7587115791303815586)
XLA Ops:
  33.5 43.2 %collective-permute-done.18 = bf16[2048,256]{1,0:T(8,128)(2,1)} collective-permute-done((bf16[2048,256]{1,0:T(8,128)(2,1)S(1)}, bf16[2048,256]{1,0:T(8,128)(2,1)}, u32[]{:S(2)}, u32[]{:S(2)}) %collective-permute-start.18) | collective-permute-done | bytes 1048608 | tf_op jit(solution)/shard_map/ppermute | solution.py:466
  94.2 43.8 %collective-permute-done.27 = bf16[1536,256]{1,0:T(8,128)(2,1)} collective-permute-done((bf16[1536,256]{1,0:T(8,128)(2,1)}, bf16[1536,256]{1,0:T(8,128)(2,1)}, u32[]{:S(2)}, u32[]{:S(2)}) %collective-permute-start.27) | collective-permute-done | bytes 786464 | tf_op jit(solution)/shard_map/ppermute | solution.py:463
  152.9 21.7 %all_gather.43 = f32[2,2,2048]{2,1,0:T(2,128)S(1)} all-gather(f32[2,2,256]{2,1,0:T(2,128)S(1)} %pad_maximum_fusion.9), channel_id=1, replica_groups=mesh['dp'=1,'tp'=4,'x'=4,'c'=2] {'x','c'}, dimensions={2}, use_global_device_ids=true | all-gather | bytes 36864 | tf_op jit(solution)/shard_map/all_gather | solution.py:540
  176.0 31.9 %qkv_raw.1 = (f32[4096,512]{1,0:T(8,128)}, f32[4096,512]{1,0:T(8,128)}, bf16[4096,512]{1,0:T(8,128)(2,1)}, f32[8,4096]{1,0:T(8,128)}) custom-call(bf16[4096,2048]{1,0:T(8,128)(2,1)} %bitcast.158, bf16[2048,1536]{1,0:T(8,128)(2,1)} %all-gather.7.cloned.1.call-done.w_ref), custom_call_target="tpu_custom_call" | custom-call | flops 25769803776 | bytes 37748736 | tf_op jit(solution)/shard_map/qkv_raw/pallas_call | solution.py:60
  219.7 13.6 %norm_rope.1 = (bf16[4096,512]{1,0:T(8,128)(2,1)}, bf16[4096,512]{1,0:T(8,128)(2,1)}) custom-call(f32[4096,512]{1,0:T(8,128)} %get-tuple-element.94.q_ref, f32[4096,512]{1,0:T(8,128)} %get-tuple-element.95.k_ref, f32[8,4096]{1,0:T(8,128)} %add_rsqrt_fusion.inv_ref, f32[1,512]{1,0:T(1,128)} %get-tuple-element.236.qg_ref, f32[1,512]{1,0:T(1,128)} %get-tuple-element.222.kg_ref, ...), custom_call_target="tpu_custom_call" | custom-call | flops 4194304000 | bytes 25165824 | tf_op jit(solution)/shard_map/norm_rope/pallas_call | solution.py:86
  233.2 22.6 %shard_map.152 = (bf16[4,512,256]{2,1,0:T(8,128)(2,1)}, bf16[4,512,256]{2,1,0:T(8,128)(2,1)}) custom-call(bf16[4,1024,512]{2,1,0:T(8,128)(2,1)} %bitcast.161, bf16[4,1024,512]{2,1,0:T(8,128)(2,1)} %bitcast.128, bf16[4,1024,512]{2,1,0:T(8,128)(2,1)} %bitcast.125), custom_call_target="tpu_custom_call" | custom-call | flops 8589934592 | bytes 12582912 | tf_op jit(solution)/shard_map/pallas_call | solution.py:138
  261.1 15.5 %shard_map.139 = (bf16[4,512,256]{2,1,0:T(8,128)(2,1)}, bf16[4,512,256]{2,1,0:T(8,128)(2,1)}) custom-call(bf16[4,1024,512]{2,1,0:T(8,128)(2,1)} %bitcast.162, bf16[4,1024,512]{2,1,0:T(8,128)(2,1)} %bitcast.129, bf16[4,1024,512]{2,1,0:T(8,128)(2,1)} %bitcast.126), custom_call_target="tpu_custom_call" | custom-call | flops 4294967296 | bytes 8388608 | tf_op jit(solution)/shard_map/pallas_call | solution.py:138
  283.5 22.4 %collective-permute-done.42.refs_2_ = bf16[4,512,256]{2,1,0:T(8,128)(2,1)} collective-permute-done((bf16[4,512,256]{2,1,0:T(8,128)(2,1)}, bf16[4,512,256]{2,1,0:T(8,128)(2,1)}, u32[]{:S(2)}, u32[]{:S(2)}) %collective-permute-start.42) | collective-permute-done | bytes 1048608 | tf_op jit(solution)/shard_map/ppermute | solution.py:466
  310.3 18.0 %collective-permute-done.7.refs_3_ = bf16[4,512,256]{2,1,0:T(8,128)(2,1)S(1)} collective-permute-done((bf16[4,512,256]{2,1,0:T(8,128)(2,1)}, bf16[4,512,256]{2,1,0:T(8,128)(2,1)S(1)}, u32[]{:S(2)}, u32[]{:S(2)}) %collective-permute-start.7) | collective-permute-done | bytes 1048608 | tf_op jit(solution)/shard_map/ppermute | solution.py:466
  331.5 19.1 %collective-permute-done.45.refs_4_ = bf16[4,512,256]{2,1,0:T(8,128)(2,1)S(1)} collective-permute-done((bf16[4,512,256]{2,1,0:T(8,128)(2,1)S(1)}, bf16[4,512,256]{2,1,0:T(8,128)(2,1)S(1)}, u32[]{:S(2)}, u32[]{:S(2)}) %collective-permute-start.45) | collective-permute-done | bytes 1048608 | tf_op jit(solution)/shard_map/ppermute | solution.py:463
  352.3 31.9 %shard_map.153 = (bf16[4,512,1024]{2,1,0:T(8,128)(2,1)}, bf16[4,512,1024]{2,1,0:T(8,128)(2,1)}) custom-call(s32[4]{0:T(128)} %compare_select_fusion.order_ref, bf16[4,512,256]{2,1,0:T(8,128)(2,1)} %get-tuple-element.132.refs_0_, bf16[4,512,256]{2,1,0:T(8,128)(2,1)} %get-tuple-element.133.refs_1_, bf16[4,512,256]{2,1,0:T(8,128)(2,1)} %collective-permute-done.42.refs_2_, ...), custom_call_target="tpu_custom_call" | custom-call | flops 17179869184 | bytes 33554432 | tf_op jit(solution)/shard_map/pallas_call | solution.py:192
  388.8 32.0 %shard_map.140 = (bf16[4,512,1024]{2,1,0:T(8,128)(2,1)}, bf16[4,512,1024]{2,1,0:T(8,128)(2,1)}) custom-call(s32[4]{0:T(128)} %compare_select_fusion.order_ref, bf16[4,512,256]{2,1,0:T(8,128)(2,1)} %get-tuple-element.100.refs_0_, bf16[4,512,256]{2,1,0:T(8,128)(2,1)} %get-tuple-element.101.refs_1_, bf16[4,512,256]{2,1,0:T(8,128)(2,1)} %collective-permute-done.6.refs_2_, ...), custom_call_target="tpu_custom_call" | custom-call | flops 17179869184 | bytes 33554432 | tf_op jit(solution)/shard_map/pallas_call | solution.py:192
  420.8 24.5 %shard_map.155.refs_1_ = bf16[2048,1024]{1,0:T(8,128)(2,1)} custom-call(bf16[4,512,1024]{2,1,0:T(8,128)(2,1)} %get-tuple-element.134.refs_0_.refs_2_.refs_4_.refs_6_, bf16[4,512,1024]{2,1,0:T(8,128)(2,1)} %get-tuple-element.135.refs_1_.refs_3_.refs_5_.refs_7_, bf16[4,512,1024]{2,1,0:T(8,128)(2,1)} %get-tuple-element.134.refs_0_.refs_2_.refs_4_.refs_6_, ...), custom_call_target="tpu_custom_call" | custom-call | flops 17179869184 | bytes 16777216 | tf_op jit(solution)/shard_map/pallas_call | solution.py:247
  445.3 24.7 %shard_map.154.refs_0_ = bf16[2048,1024]{1,0:T(8,128)(2,1)} custom-call(bf16[4,512,1024]{2,1,0:T(8,128)(2,1)} %get-tuple-element.134.refs_0_.refs_2_.refs_4_.refs_6_, bf16[4,512,1024]{2,1,0:T(8,128)(2,1)} %get-tuple-element.135.refs_1_.refs_3_.refs_5_.refs_7_, bf16[4,512,1024]{2,1,0:T(8,128)(2,1)} %get-tuple-element.134.refs_0_.refs_2_.refs_4_.refs_6_, ...), custom_call_target="tpu_custom_call" | custom-call | flops 17179869184 | bytes 16777216 | tf_op jit(solution)/shard_map/pallas_call | solution.py:247
  470.0 43.8 %shard_map.156 = (bf16[512,1024]{1,0:T(8,128)(2,1)}, bf16[512,1024]{1,0:T(8,128)(2,1)}, bf16[512,1024]{1,0:T(8,128)(2,1)}, bf16[512,1024]{1,0:T(8,128)(2,1)}, bf...) custom-call(bf16[2048,1024]{1,0:T(8,128)(2,1)} %shard_map.154.refs_0, ...), custom_call_target="tpu_custom_call" | custom-call | flops 17179869184 | bytes 25165824 | tf_op jit(solution)/shard_map/pallas_call | solution.py:299
  520.1 24.3 %shard_map.142.refs_1_ = bf16[2048,1024]{1,0:T(8,128)(2,1)} custom-call(bf16[4,512,1024]{2,1,0:T(8,128)(2,1)} %get-tuple-element.103.refs_0_.refs_2_.refs_4_.refs_6_, bf16[4,512,1024]{2,1,0:T(8,128)(2,1)} %get-tuple-element.104.refs_1_.refs_3_.refs_5_.refs_7_, bf16[4,512,1024]{2,1,0:T(8,128)(2,1)} %get-tuple-element.103.refs_0_.refs_2_.refs_4_.refs_6_, ...), custom_call_target="tpu_custom_call" | custom-call | flops 17179869184 | bytes 16777216 | tf_op jit(solution)/shard_map/pallas_call | solution.py:247
  544.4 24.6 %shard_map.141.refs_0_ = bf16[2048,1024]{1,0:T(8,128)(2,1)} custom-call(bf16[4,512,1024]{2,1,0:T(8,128)(2,1)} %get-tuple-element.103.refs_0_.refs_2_.refs_4_.refs_6_, bf16[4,512,1024]{2,1,0:T(8,128)(2,1)} %get-tuple-element.104.refs_1_.refs_3_.refs_5_.refs_7_, bf16[4,512,1024]{2,1,0:T(8,128)(2,1)} %get-tuple-element.103.refs_0_.refs_2_.refs_4_.refs_6_, ...), custom_call_target="tpu_custom_call" | custom-call | flops 17179869184 | bytes 16777216 | tf_op jit(solution)/shard_map/pallas_call | solution.py:247
  576.6 43.9 %shard_map.143 = (bf16[512,1024]{1,0:T(8,128)(2,1)}, bf16[512,1024]{1,0:T(8,128)(2,1)}, bf16[512,1024]{1,0:T(8,128)(2,1)}, bf16[512,1024]{1,0:T(8,128)(2,1)}, bf...) custom-call(bf16[2048,1024]{1,0:T(8,128)(2,1)} %shard_map.141.refs_0, ...), custom_call_target="tpu_custom_call" | custom-call | flops 17179869184 | bytes 25165824 | tf_op jit(solution)/shard_map/pallas_call | solution.py:299
  630.9 22.1 %shard_map.158 = (bf16[4,512,512]{2,1,0:T(8,128)(2,1)}, bf16[4,512,512]{2,1,0:T(8,128)(2,1)}, bf16[4,512,512]{2,1,0:T(8,128)(2,1)}) custom-call(bf16[512,2048]{1,0:T(8,128)(2,1)} %shard_map.157.x_ref, bf16[8,4,2048,256]{3,2,1,0:T(8,128)(2,1)} %all-gather.15.cloned.1.call-done.w_ref, f32[1,2048]{1,0:T(1,128)} %bitcast.139, f32[1,2048]{1,0:T(1,128)} %bitcast.141, ...), custom_call_target="tpu_custom_call" | custom-call | flops 12884901888 | bytes 33554432 | tf_op jit(solution)/shard_map/pallas_call | solution.py:396
  669.7 15.7 %all-to-all-done.2 = bf16[4,512,512]{2,1,0:T(8,128)(2,1)S(1)} async-done(((bf16[4,512,512]{2,1,0:T(8,128)(2,1)}), bf16[4,512,512]{2,1,0:T(8,128)(2,1)S(1)}, u32[]{:S(2)}, u32[]{:S(2)}) %all-to-all-start.2) | async-done | bytes 2097184 | tf_op jit(solution)/shard_map/all_to_all | solution.py:600
  689.9 16.5 %collective-permute-done.14.refs_2_ = bf16[512,1024]{1,0:T(8,128)(2,1)} collective-permute-done((bf16[512,1024]{1,0:T(8,128)(2,1)}, bf16[512,1024]{1,0:T(8,128)(2,1)}, u32[]{:S(2)}, u32[]{:S(2)}) %collective-permute-start.14) | collective-permute-done | bytes 1048608 | tf_op jit(solution)/shard_map/ppermute | solution.py:466
  706.4 22.5 %collective-permute-done.17.refs_5_ = bf16[512,1024]{1,0:T(8,128)(2,1)} collective-permute-done((bf16[512,1024]{1,0:T(8,128)(2,1)}, bf16[512,1024]{1,0:T(8,128)(2,1)}, u32[]{:S(2)}, u32[]{:S(2)}) %collective-permute-start.17) | collective-permute-done | bytes 1048608 | tf_op jit(solution)/shard_map/ppermute | solution.py:466
  736.7 22.0 %shard_map.145 = (bf16[4,512,512]{2,1,0:T(8,128)(2,1)}, bf16[4,512,512]{2,1,0:T(8,128)(2,1)}, bf16[4,512,512]{2,1,0:T(8,128)(2,1)}) custom-call(bf16[512,2048]{1,0:T(8,128)(2,1)} %shard_map.144.x_ref, bf16[8,4,2048,256]{3,2,1,0:T(8,128)(2,1)} %all-gather.15.cloned.1.call-done.w_ref, f32[1,2048]{1,0:T(1,128)} %bitcast.140, f32[1,2048]{1,0:T(1,128)} %bitcast.142, ...), custom_call_target="tpu_custom_call" | custom-call | flops 12884901888 | bytes 33554432 | tf_op jit(solution)/shard_map/pallas_call | solution.py:396
  762.6 22.2 %shard_map.159 = (bf16[4,512,256]{2,1,0:T(8,128)(2,1)}, bf16[4,512,256]{2,1,0:T(8,128)(2,1)}) custom-call(bf16[4,512,512]{2,1,0:T(8,128)(2,1)} %get-tuple-element.144.q_ref, bf16[4,512,512]{2,1,0:T(8,128)(2,1)} %get-tuple-element.116.refs_0_, bf16[4,512,512]{2,1,0:T(8,128)(2,1)} %get-tuple-element.145.refs_1_, ...), custom_call_target="tpu_custom_call" | custom-call | flops 8589934592 | bytes 12582912 | tf_op jit(solution)/shard_map/pallas_call | solution.py:138
  784.8 11.1 shard_map.160
  804.7 15.5 %shard_map.146 = (bf16[4,512,256]{2,1,0:T(8,128)(2,1)}, bf16[4,512,256]{2,1,0:T(8,128)(2,1)}) custom-call(bf16[4,512,512]{2,1,0:T(8,128)(2,1)} %get-tuple-element.115.q_ref, bf16[4,512,512]{2,1,0:T(8,128)(2,1)} %get-tuple-element.116.refs_0_, bf16[4,512,512]{2,1,0:T(8,128)(2,1)} %get-tuple-element.117.refs_1_.refs_2_), custom_call_target="tpu_custom_call" | custom-call | flops 4294967296 | bytes 8388608 | tf_op jit(solution)/shard_map/pallas_call | solution.py:138
  820.2 11.1 shard_map.147
  841.4 19.3 %collective-permute-done.23.refs_6_ = bf16[512,1024]{1,0:T(8,128)(2,1)} collective-permute-done((bf16[512,1024]{1,0:T(8,128)(2,1)}, bf16[512,1024]{1,0:T(8,128)(2,1)}, u32[]{:S(2)}, u32[]{:S(2)}) %collective-permute-start.23) | collective-permute-done | bytes 1048608 | tf_op jit(solution)/shard_map/ppermute | solution.py:463
  865.2 17.9 %collective-permute-done.57.refs_4_ = bf16[512,1024]{1,0:T(8,128)(2,1)S(1)} collective-permute-done((bf16[512,1024]{1,0:T(8,128)(2,1)S(1)}, bf16[512,1024]{1,0:T(8,128)(2,1)S(1)}, u32[]{:S(2)}, u32[]{:S(2)}) %collective-permute-start.57) | collective-permute-done | bytes 1048608 | tf_op jit(solution)/shard_map/ppermute | solution.py:463
  885.0 24.6 %shard_map.162.refs_1_ = bf16[2048,1024]{1,0:T(8,128)(2,1)} custom-call(bf16[512,1024]{1,0:T(8,128)(2,1)} %get-tuple-element.151.refs_0_, bf16[512,1024]{1,0:T(8,128)(2,1)} %get-tuple-element.152.refs_1_, bf16[512,1024]{1,0:T(8,128)(2,1)} %collective-permute-done.54.refs_2_, bf16[512,1024]{1,0:T(8,128)(2,1)} %collective-permute-done.55.refs_3_, ...), custom_call_target="tpu_custom_call" | custom-call | flops 17179869184 | bytes 16777216 | tf_op jit(solution)/shard_map/pallas_call | solution.py:247
  909.6 24.3 %shard_map.161.refs_0_ = bf16[2048,1024]{1,0:T(8,128)(2,1)} custom-call(bf16[512,1024]{1,0:T(8,128)(2,1)} %get-tuple-element.151.refs_0_, bf16[512,1024]{1,0:T(8,128)(2,1)} %get-tuple-element.152.refs_1_, bf16[512,1024]{1,0:T(8,128)(2,1)} %collective-permute-done.54.refs_2_, bf16[512,1024]{1,0:T(8,128)(2,1)} %collective-permute-done.55.refs_3_, ...), custom_call_target="tpu_custom_call" | custom-call | flops 17179869184 | bytes 16777216 | tf_op jit(solution)/shard_map/pallas_call | solution.py:247
  934.0 24.3 %shard_map.149.refs_1_ = bf16[2048,1024]{1,0:T(8,128)(2,1)} custom-call(bf16[512,1024]{1,0:T(8,128)(2,1)} %get-tuple-element.120.refs_0_, bf16[512,1024]{1,0:T(8,128)(2,1)} %get-tuple-element.121.refs_1_, bf16[512,1024]{1,0:T(8,128)(2,1)} %collective-permute-done.21.refs_2_, bf16[512,1024]{1,0:T(8,128)(2,1)} %collective-permute-done.22.refs_3_, ...), custom_call_target="tpu_custom_call" | custom-call | flops 17179869184 | bytes 16777216 | tf_op jit(solution)/shard_map/pallas_call | solution.py:247
  958.2 24.2 %shard_map.148.refs_0_ = bf16[2048,1024]{1,0:T(8,128)(2,1)} custom-call(bf16[512,1024]{1,0:T(8,128)(2,1)} %get-tuple-element.120.refs_0_, bf16[512,1024]{1,0:T(8,128)(2,1)} %get-tuple-element.121.refs_1_, bf16[512,1024]{1,0:T(8,128)(2,1)} %collective-permute-done.21.refs_2_, bf16[512,1024]{1,0:T(8,128)(2,1)} %collective-permute-done.22.refs_3_, ...), custom_call_target="tpu_custom_call" | custom-call | flops 17179869184 | bytes 16777216 | tf_op jit(solution)/shard_map/pallas_call | solution.py:247
  982.5 44.1 %shard_map.150 = (bf16[512,1024]{1,0:T(8,128)(2,1)}, bf16[512,1024]{1,0:T(8,128)(2,1)}, bf16[512,1024]{1,0:T(8,128)(2,1)}, bf16[512,1024]{1,0:T(8,128)(2,1)}, bf...) custom-call(bf16[2048,1024]{1,0:T(8,128)(2,1)} %shard_map.148.refs_0, ...), custom_call_target="tpu_custom_call" | custom-call | flops 17179869184 | bytes 25165824 | tf_op jit(solution)/shard_map/pallas_call | solution.py:299
  1029.6 43.6 %shard_map.163 = (bf16[512,1024]{1,0:T(8,128)(2,1)}, bf16[512,1024]{1,0:T(8,128)(2,1)}, bf16[512,1024]{1,0:T(8,128)(2,1)}, bf16[512,1024]{1,0:T(8,128)(2,1)}, bf...) custom-call(bf16[2048,1024]{1,0:T(8,128)(2,1)} %shard_map.161.refs_0, ...), custom_call_target="tpu_custom_call" | custom-call | flops 17179869184 | bytes 25165824 | tf_op jit(solution)/shard_map/pallas_call | solution.py:299
  1084.4 15.8 %collective-permute-done.64 = bf16[512,1024]{1,0:T(8,128)(2,1)S(1)} collective-permute-done((bf16[512,1024]{1,0:T(8,128)(2,1)}, bf16[512,1024]{1,0:T(8,128)(2,1)S(1)}, u32[]{:S(2)}, u32[]{:S(2)}) %collective-permute-start.64) | collective-permute-done | bytes 1048608 | tf_op jit(solution)/shard_map/ppermute | solution.py:466
  1106.2 16.4 %collective-permute-done.32.refs_2_ = bf16[512,1024]{1,0:T(8,128)(2,1)S(1)} collective-permute-done((bf16[512,1024]{1,0:T(8,128)(2,1)}, bf16[512,1024]{1,0:T(8,128)(2,1)S(1)}, u32[]{:S(2)}, u32[]{:S(2)}) %collective-permute-start.32) | collective-permute-done | bytes 1048608 | tf_op jit(solution)/shard_map/ppermute | solution.py:466
  1125.9 19.3 %collective-permute-done.35.refs_5_ = bf16[512,1024]{1,0:T(8,128)(2,1)} collective-permute-done((bf16[512,1024]{1,0:T(8,128)(2,1)S(1)}, bf16[512,1024]{1,0:T(8,128)(2,1)}, u32[]{:S(2)}, u32[]{:S(2)}) %collective-permute-start.35) | collective-permute-done | bytes 1048608 | tf_op jit(solution)/shard_map/ppermute | solution.py:466
  1156.7 6.9 reshape.74
  1163.6 7.0 reshape.75
  1193.5 6.9 reshape.76
  1200.4 7.1 reshape.77
  1212.0 9.1 pad_maximum_fusion.1
  1221.1 7.2 pad_maximum_fusion
  1238.9 17.3 %collective-permute-done.39 = bf16[512,1024]{1,0:T(8,128)(2,1)S(1)} collective-permute-done((bf16[512,1024]{1,0:T(8,128)(2,1)}, bf16[512,1024]{1,0:T(8,128)(2,1)S(1)}, u32[]{:S(2)}, u32[]{:S(2)}) %collective-permute-start.39) | collective-permute-done | bytes 1048608 | tf_op jit(solution)/shard_map/ppermute | solution.py:463
  1259.9 14.6 %collective-permute-done.40 = bf16[512,1024]{1,0:T(8,128)(2,1)S(1)} collective-permute-done((bf16[512,1024]{1,0:T(8,128)(2,1)S(1)}, bf16[512,1024]{1,0:T(8,128)(2,1)S(1)}, u32[]{:S(2)}, u32[]{:S(2)}) %collective-permute-start.40) | collective-permute-done | bytes 1048608 | tf_op jit(solution)/shard_map/ppermute | solution.py:466
  1279.3 6.4 collective-permute-done.66
  1286.0 17.9 %collective-permute-done.69 = bf16[512,1024]{1,0:T(8,128)(2,1)S(1)} collective-permute-done((bf16[512,1024]{1,0:T(8,128)(2,1)S(1)}, bf16[512,1024]{1,0:T(8,128)(2,1)S(1)}, u32[]{:S(2)}, u32[]{:S(2)}) %collective-permute-start.69) | collective-permute-done | bytes 1048608 | tf_op jit(solution)/shard_map/ppermute | solution.py:463
  (297 shorter events, 260.4 us)
Async XLA Ops:
  7.2 168.8 %all-gather.7.cloned.1.call-start = ((), (), s32[]{:S(2)}) async-start(), calls=%async_computation.4 | async-start | bytes 7077888 | tf_op jit(solution)/shard_map/all_gather | solution.py:539
  11.4 340.9 %all-gather.9.cloned.1.call-start = ((), (), s32[]{:S(2)}) async-start(), calls=%async_computation.5 | async-start | bytes 8650752 | tf_op jit(solution)/shard_map/all_gather | solution.py:520
  12.3 408.5 %all-gather.11.cloned.1.call-start = ((), (), s32[]{:S(2)}) async-start(), calls=%async_computation.6 | async-start | bytes 18874368 | tf_op jit(solution)/shard_map/all_gather | solution.py:545
  16.5 453.5 %all-gather.13.cloned.1.call-start = ((), (), s32[]{:S(2)}) async-start(), calls=%async_computation.7 | async-start | bytes 9437184 | tf_op jit(solution)/shard_map/all_gather | solution.py:546
  19.0 611.9 %all-gather.15.cloned.1.call-start = ((), (), s32[]{:S(2)}) async-start(), calls=%async_computation.8 | async-start | bytes 37748736 | tf_op jit(solution)/shard_map/all_gather | solution.py:549
  23.8 52.9 %collective-permute-start.18 = (bf16[2048,256]{1,0:T(8,128)(2,1)S(1)}, bf16[2048,256]{1,0:T(8,128)(2,1)}, u32[]{:S(2)}, u32[]{:S(2)}) collective-permute-start(bf16[2048,256]{1,0:T(8,128)(2,1)S(1)} %bitcast_dynamic-update-slice_fusion.28), channel_id=1, source_target_pairs={{0,24},{8,0},{16,8},{24,16},{1,25},{9,1},{17,9},{25,17},{2,26},{10... | collective-permute-start | bytes 3145736 | tf_op jit(solution)/shard_map/ppermute | solution.py:466
  28.5 50.5 %collective-permute-start.19 = (bf16[2048,256]{1,0:T(8,128)(2,1)S(1)}, bf16[2048,256]{1,0:T(8,128)(2,1)}, u32[]{:S(2)}, u32[]{:S(2)}) collective-permute-start(bf16[2048,256]{1,0:T(8,128)(2,1)S(1)} %bitcast_dynamic-update-slice_fusion.28), channel_id=1, source_target_pairs={{0,8},{8,16},{16,24},{24,0},{1,9},{9,17},{17,25},{25,1},{2,10},{10... | collective-permute-start | bytes 3145736 | tf_op jit(solution)/shard_map/ppermute | solution.py:463
  28.5 52.7 %collective-permute-start.20 = (bf16[2048,256]{1,0:T(8,128)(2,1)S(1)}, bf16[2048,256]{1,0:T(8,128)(2,1)}, u32[]{:S(2)}, u32[]{:S(2)}) collective-permute-start(bf16[2048,256]{1,0:T(8,128)(2,1)S(1)} %bitcast_dynamic-update-slice_fusion.28), channel_id=1, source_target_pairs={{0,16},{8,24},{16,0},{24,8},{1,17},{9,25},{17,1},{25,9},{2,18},{10... | collective-permute-start | bytes 3145736 | tf_op jit(solution)/shard_map/ppermute | solution.py:469
  83.6 801.4 %all-gather.17.cloned.1.call-start = ((), (), s32[]{:S(2)}) async-start(), calls=%async_computation.9 | async-start | bytes 28311552 | tf_op jit(solution)/shard_map/all_gather | solution.py:555
  87.3 50.7 %collective-permute-start.27 = (bf16[1536,256]{1,0:T(8,128)(2,1)}, bf16[1536,256]{1,0:T(8,128)(2,1)}, u32[]{:S(2)}, u32[]{:S(2)}) collective-permute-start(bf16[1536,256]{1,0:T(8,128)(2,1)} %get-tuple-element.185), channel_id=1, source_target_pairs={{0,2},{2,4},{4,6},{6,0},{1,3},{3,5},{5,7},{7,1},{8,10},{10,12},{12... | collective-permute-start | bytes 2359304 | tf_op jit(solution)/shard_map/ppermute | solution.py:463
  88.6 51.5 %collective-permute-start.28 = (bf16[1536,256]{1,0:T(8,128)(2,1)}, bf16[1536,256]{1,0:T(8,128)(2,1)}, u32[]{:S(2)}, u32[]{:S(2)}) collective-permute-start(bf16[1536,256]{1,0:T(8,128)(2,1)} %get-tuple-element.184), channel_id=1, source_target_pairs={{0,6},{2,0},{4,2},{6,4},{1,7},{3,1},{5,3},{7,5},{8,14},{10,8},{12,... | collective-permute-start | bytes 2359304 | tf_op jit(solution)/shard_map/ppermute | solution.py:466
  89.3 52.9 %collective-permute-start.29 = (bf16[1536,256]{1,0:T(8,128)(2,1)}, bf16[1536,256]{1,0:T(8,128)(2,1)}, u32[]{:S(2)}, u32[]{:S(2)}) collective-permute-start(bf16[1536,256]{1,0:T(8,128)(2,1)} %get-tuple-element.183), channel_id=1, source_target_pairs={{0,4},{2,6},{4,0},{6,2},{1,5},{3,7},{5,1},{7,3},{8,12},{10,14},{12... | collective-permute-start | bytes 2359304 | tf_op jit(solution)/shard_map/ppermute | solution.py:469
  259.0 46.9 %collective-permute-start.42 = (bf16[4,512,256]{2,1,0:T(8,128)(2,1)}, bf16[4,512,256]{2,1,0:T(8,128)(2,1)}, u32[]{:S(2)}, u32[]{:S(2)}) collective-permute-start(bf16[4,512,256]{2,1,0:T(8,128)(2,1)} %get-tuple-element.132.refs_0_), channel_id=1, source_target_pairs={{0,24},{8,0},{16,8},{24,16},{1,25},{9,1},{17,9},{25,17},{2,26},{10... | collective-permute-start | bytes 3145736 | tf_op jit(solution)/shard_map/ppermute | solution.py:466
  259.7 50.6 %collective-permute-start.47 = (bf16[4,512,256]{2,1,0:T(8,128)(2,1)}, bf16[4,512,256]{2,1,0:T(8,128)(2,1)}, u32[]{:S(2)}, u32[]{:S(2)}) collective-permute-start(bf16[4,512,256]{2,1,0:T(8,128)(2,1)} %get-tuple-element.133.refs_1_), channel_id=1, source_target_pairs={{0,8},{8,16},{16,24},{24,0},{1,9},{9,17},{17,25},{25,1},{2,10},{10... | collective-permute-start | bytes 3145736 | tf_op jit(solution)/shard_map/ppermute | solution.py:463
  276.6 51.7 %collective-permute-start.7 = (bf16[4,512,256]{2,1,0:T(8,128)(2,1)}, bf16[4,512,256]{2,1,0:T(8,128)(2,1)S(1)}, u32[]{:S(2)}, u32[]{:S(2)}) collective-permute-start(bf16[4,512,256]{2,1,0:T(8,128)(2,1)} %get-tuple-element.101.refs_1_), channel_id=1, source_target_pairs={{0,24},{8,0},{16,8},{24,16},{1,25},{9,1},{17,9},{25,17},{2,26},{10... | collective-permute-start | bytes 3145736 | tf_op jit(solution)/shard_map/ppermute | solution.py:466
  283.3 48.2 %collective-permute-start.8 = (bf16[4,512,256]{2,1,0:T(8,128)(2,1)}, bf16[4,512,256]{2,1,0:T(8,128)(2,1)}, u32[]{:S(2)}, u32[]{:S(2)}) collective-permute-start(bf16[4,512,256]{2,1,0:T(8,128)(2,1)} %get-tuple-element.100.refs_0_), channel_id=1, source_target_pairs={{0,8},{8,16},{16,24},{24,0},{1,9},{9,17},{17,25},{25,1},{2,10},{10... | collective-permute-start | bytes 3145736 | tf_op jit(solution)/shard_map/ppermute | solution.py:463
  283.5 67.2 %collective-permute-start.45 = (bf16[4,512,256]{2,1,0:T(8,128)(2,1)S(1)}, bf16[4,512,256]{2,1,0:T(8,128)(2,1)S(1)}, u32[]{:S(2)}, u32[]{:S(2)}) collective-permute-start(bf16[4,512,256]{2,1,0:T(8,128)(2,1)S(1)} %collective-permute-done.44.refs_6_), channel_id=1, source_target_pairs={{0,8},{8,16},{16,24},{24,0},{1,9},{9,17},{17,25},{25,1},{2,10},{10... | collective-permute-start | bytes 3145736 | tf_op jit(solution)/shard_map/ppermute | solution.py:463
  310.3 74.0 %collective-permute-start.11 = (bf16[4,512,256]{2,1,0:T(8,128)(2,1)}, bf16[4,512,256]{2,1,0:T(8,128)(2,1)}, u32[]{:S(2)}, u32[]{:S(2)}) collective-permute-start(bf16[4,512,256]{2,1,0:T(8,128)(2,1)} %get-tuple-element.101.refs_1_), channel_id=1, source_target_pairs={{0,8},{8,16},{16,24},{24,0},{1,9},{9,17},{17,25},{25,1},{2,10},{10... | collective-permute-start | bytes 3145736 | tf_op jit(solution)/shard_map/ppermute | solution.py:463
  328.3 56.0 %collective-permute-start.6 = (bf16[4,512,256]{2,1,0:T(8,128)(2,1)}, bf16[4,512,256]{2,1,0:T(8,128)(2,1)}, u32[]{:S(2)}, u32[]{:S(2)}) collective-permute-start(bf16[4,512,256]{2,1,0:T(8,128)(2,1)} %get-tuple-element.100.refs_0_), channel_id=1, source_target_pairs={{0,24},{8,0},{16,8},{24,16},{1,25},{9,1},{17,9},{25,17},{2,26},{10... | collective-permute-start | bytes 3145736 | tf_op jit(solution)/shard_map/ppermute | solution.py:466
  331.4 57.3 %collective-permute-start.10 = (bf16[4,512,256]{2,1,0:T(8,128)(2,1)S(1)}, bf16[4,512,256]{2,1,0:T(8,128)(2,1)}, u32[]{:S(2)}, u32[]{:S(2)}) collective-permute-start(bf16[4,512,256]{2,1,0:T(8,128)(2,1)S(1)} %collective-permute-done.7.refs_3_), channel_id=1, source_target_pairs={{0,24},{8,0},{16,8},{24,16},{1,25},{9,1},{17,9},{25,17},{2,26},{10... | collective-permute-start | bytes 3145736 | tf_op jit(solution)/shard_map/ppermute | solution.py:466
  513.8 55.2 %collective-permute-start.52 = (bf16[512,1024]{1,0:T(8,128)(2,1)}, bf16[512,1024]{1,0:T(8,128)(2,1)S(1)}, u32[]{:S(2)}, u32[]{:S(2)}) collective-permute-start(bf16[512,1024]{1,0:T(8,128)(2,1)} %get-tuple-element.143), channel_id=1, source_target_pairs={{0,24},{8,0},{16,8},{24,16},{1,25},{9,1},{17,9},{25,17},{2,26},{10... | collective-permute-start | bytes 3145736 | tf_op jit(solution)/shard_map/ppermute | solution.py:466
  516.8 58.0 %collective-permute-start.48 = (bf16[512,1024]{1,0:T(8,128)(2,1)}, bf16[512,1024]{1,0:T(8,128)(2,1)}, u32[]{:S(2)}, u32[]{:S(2)}) collective-permute-start(bf16[512,1024]{1,0:T(8,128)(2,1)} %get-tuple-element.138), channel_id=1, source_target_pairs={{0,8},{8,16},{16,24},{24,0},{1,9},{9,17},{17,25},{25,1},{2,10},{10... | collective-permute-start | bytes 3145736 | tf_op jit(solution)/shard_map/ppermute | solution.py:463
  516.8 107.0 %collective-permute-start.50 = (bf16[512,1024]{1,0:T(8,128)(2,1)}, bf16[512,1024]{1,0:T(8,128)(2,1)}, u32[]{:S(2)}, u32[]{:S(2)}) collective-permute-start(bf16[512,1024]{1,0:T(8,128)(2,1)} %get-tuple-element.139), channel_id=1, source_target_pairs={{0,24},{8,0},{16,8},{24,16},{1,25},{9,1},{17,9},{25,17},{2,26},{10... | collective-permute-start | bytes 3145736 | tf_op jit(solution)/shard_map/ppermute | solution.py:466
  520.1 103.7 %collective-permute-start.51 = (bf16[512,1024]{1,0:T(8,128)(2,1)}, bf16[512,1024]{1,0:T(8,128)(2,1)}, u32[]{:S(2)}, u32[]{:S(2)}) collective-permute-start(bf16[512,1024]{1,0:T(8,128)(2,1)} %get-tuple-element.141), channel_id=1, source_target_pairs={{0,8},{8,16},{16,24},{24,0},{1,9},{9,17},{17,25},{25,1},{2,10},{10... | collective-permute-start | bytes 3145736 | tf_op jit(solution)/shard_map/ppermute | solution.py:463
  571.6 52.2 %collective-permute-start.53 = (bf16[512,1024]{1,0:T(8,128)(2,1)S(1)}, bf16[512,1024]{1,0:T(8,128)(2,1)}, u32[]{:S(2)}, u32[]{:S(2)}) collective-permute-start(bf16[512,1024]{1,0:T(8,128)(2,1)S(1)} %add.159), channel_id=1, source_target_pairs={{0,24},{8,0},{16,8},{24,16},{1,25},{9,1},{17,9},{25,17},{2,26},{10... | collective-permute-start | bytes 3145736 | tf_op jit(solution)/shard_map/ppermute | solution.py:466
  576.5 47.4 %collective-permute-start.49 = (bf16[512,1024]{1,0:T(8,128)(2,1)S(1)}, bf16[512,1024]{1,0:T(8,128)(2,1)S(1)}, u32[]{:S(2)}, u32[]{:S(2)}) collective-permute-start(bf16[512,1024]{1,0:T(8,128)(2,1)S(1)} %add.158), channel_id=1, source_target_pairs={{0,8},{8,16},{16,24},{24,0},{1,9},{9,17},{17,25},{25,1},{2,10},{10... | collective-permute-start | bytes 3145736 | tf_op jit(solution)/shard_map/ppermute | solution.py:463
  657.6 48.8 %collective-permute-start.14 = (bf16[512,1024]{1,0:T(8,128)(2,1)}, bf16[512,1024]{1,0:T(8,128)(2,1)}, u32[]{:S(2)}, u32[]{:S(2)}) collective-permute-start(bf16[512,1024]{1,0:T(8,128)(2,1)} %get-tuple-element.108), channel_id=1, source_target_pairs={{0,24},{8,0},{16,8},{24,16},{1,25},{9,1},{17,9},{25,17},{2,26},{10... | collective-permute-start | bytes 3145736 | tf_op jit(solution)/shard_map/ppermute | solution.py:466
  663.8 65.1 %collective-permute-start.17 = (bf16[512,1024]{1,0:T(8,128)(2,1)}, bf16[512,1024]{1,0:T(8,128)(2,1)}, u32[]{:S(2)}, u32[]{:S(2)}) collective-permute-start(bf16[512,1024]{1,0:T(8,128)(2,1)} %add.144), channel_id=1, source_target_pairs={{0,24},{8,0},{16,8},{24,16},{1,25},{9,1},{17,9},{25,17},{2,26},{10... | collective-permute-start | bytes 3145736 | tf_op jit(solution)/shard_map/ppermute | solution.py:466
  669.7 60.0 %collective-permute-start.13 = (bf16[512,1024]{1,0:T(8,128)(2,1)}, bf16[512,1024]{1,0:T(8,128)(2,1)S(1)}, u32[]{:S(2)}, u32[]{:S(2)}) collective-permute-start(bf16[512,1024]{1,0:T(8,128)(2,1)} %add.143), channel_id=1, source_target_pairs={{0,8},{8,16},{16,24},{24,0},{1,9},{9,17},{17,25},{25,1},{2,10},{10... | collective-permute-start | bytes 3145736 | tf_op jit(solution)/shard_map/ppermute | solution.py:463
  685.4 73.3 %all-to-all-start.3 = ((bf16[4,512,512]{2,1,0:T(8,128)(2,1)}), bf16[4,512,512]{2,1,0:T(8,128)(2,1)}, u32[]{:S(2)}, u32[]{:S(2)}) async-start(bf16[4,512,512]{2,1,0:T(8,128)(2,1)} %get-tuple-element.146.refs_3_), calls=%async_computation.3 | async-start | bytes 4194304 | tf_op jit(solution)/shard_map/all_to_all | solution.py:600
  799.9 85.0 %all-to-all-start.1 = ((bf16[4,512,512]{2,1,0:T(8,128)(2,1)}), bf16[4,512,512]{2,1,0:T(8,128)(2,1)}, u32[]{:S(2)}, u32[]{:S(2)}) async-start(bf16[4,512,512]{2,1,0:T(8,128)(2,1)} %get-tuple-element.117.refs_1_.refs_2_), calls=%async_computation.1 | async-start | bytes 4194304 | tf_op jit(solution)/shard_map/all_to_all | solution.py:600
  834.0 49.0 %collective-permute-start.57 = (bf16[512,1024]{1,0:T(8,128)(2,1)S(1)}, bf16[512,1024]{1,0:T(8,128)(2,1)S(1)}, u32[]{:S(2)}, u32[]{:S(2)}) collective-permute-start(bf16[512,1024]{1,0:T(8,128)(2,1)S(1)} %collective-permute-done.56.refs_6_), channel_id=1, source_target_pairs={{0,2},{2,4},{4,6},{6,0},{1,3},{3,5},{5,7},{7,1},{8,10},{10,12},{12... | collective-permute-start | bytes 3145736 | tf_op jit(solution)/shard_map/ppermute | solution.py:463
  839.5 94.5 %collective-permute-start.21 = (bf16[512,1024]{1,0:T(8,128)(2,1)}, bf16[512,1024]{1,0:T(8,128)(2,1)}, u32[]{:S(2)}, u32[]{:S(2)}) collective-permute-start(bf16[512,1024]{1,0:T(8,128)(2,1)} %get-tuple-element.120.refs_0_), channel_id=1, source_target_pairs={{0,6},{2,0},{4,2},{6,4},{1,7},{3,1},{5,3},{7,5},{8,14},{10,8},{12,... | collective-permute-start | bytes 3145736 | tf_op jit(solution)/shard_map/ppermute | solution.py:466
  860.7 73.2 %collective-permute-start.26 = (bf16[512,1024]{1,0:T(8,128)(2,1)}, bf16[512,1024]{1,0:T(8,128)(2,1)}, u32[]{:S(2)}, u32[]{:S(2)}) collective-permute-start(bf16[512,1024]{1,0:T(8,128)(2,1)} %get-tuple-element.121.refs_1_), channel_id=1, source_target_pairs={{0,2},{2,4},{4,6},{6,0},{1,3},{3,5},{5,7},{7,1},{8,10},{10,12},{12... | collective-permute-start | bytes 3145736 | tf_op jit(solution)/shard_map/ppermute | solution.py:463
  861.9 72.0 %collective-permute-start.24 = (bf16[512,1024]{1,0:T(8,128)(2,1)}, bf16[512,1024]{1,0:T(8,128)(2,1)}, u32[]{:S(2)}, u32[]{:S(2)}) collective-permute-start(bf16[512,1024]{1,0:T(8,128)(2,1)} %collective-permute-done.23.refs_6_), channel_id=1, source_target_pairs={{0,2},{2,4},{4,6},{6,0},{1,3},{3,5},{5,7},{7,1},{8,10},{10,12},{12... | collective-permute-start | bytes 3145736 | tf_op jit(solution)/shard_map/ppermute | solution.py:463
  884.0 49.9 %collective-permute-start.25 = (bf16[512,1024]{1,0:T(8,128)(2,1)}, bf16[512,1024]{1,0:T(8,128)(2,1)}, u32[]{:S(2)}, u32[]{:S(2)}) collective-permute-start(bf16[512,1024]{1,0:T(8,128)(2,1)} %collective-permute-done.22.refs_3_), channel_id=1, source_target_pairs={{0,6},{2,0},{4,2},{6,4},{1,7},{3,1},{5,3},{7,5},{8,14},{10,8},{12,... | collective-permute-start | bytes 3145736 | tf_op jit(solution)/shard_map/ppermute | solution.py:466
  1026.5 50.8 %collective-permute-start.34 = (bf16[512,1024]{1,0:T(8,128)(2,1)}, bf16[512,1024]{1,0:T(8,128)(2,1)}, u32[]{:S(2)}, u32[]{:S(2)}) collective-permute-start(bf16[512,1024]{1,0:T(8,128)(2,1)} %get-tuple-element.129), channel_id=1, source_target_pairs={{0,6},{2,0},{4,2},{6,4},{1,7},{3,1},{5,3},{7,5},{8,14},{10,8},{12,... | collective-permute-start | bytes 3145736 | tf_op jit(solution)/shard_map/ppermute | solution.py:466
  1029.6 51.6 %collective-permute-start.30 = (bf16[512,1024]{1,0:T(8,128)(2,1)}, bf16[512,1024]{1,0:T(8,128)(2,1)}, u32[]{:S(2)}, u32[]{:S(2)}) collective-permute-start(bf16[512,1024]{1,0:T(8,128)(2,1)} %get-tuple-element.124), channel_id=1, source_target_pairs={{0,2},{2,4},{4,6},{6,0},{1,3},{3,5},{5,7},{7,1},{8,10},{10,12},{12... | collective-permute-start | bytes 3145736 | tf_op jit(solution)/shard_map/ppermute | solution.py:463
  1076.1 46.6 %collective-permute-start.32 = (bf16[512,1024]{1,0:T(8,128)(2,1)}, bf16[512,1024]{1,0:T(8,128)(2,1)S(1)}, u32[]{:S(2)}, u32[]{:S(2)}) collective-permute-start(bf16[512,1024]{1,0:T(8,128)(2,1)} %get-tuple-element.125), channel_id=1, source_target_pairs={{0,6},{2,0},{4,2},{6,4},{1,7},{3,1},{5,3},{7,5},{8,14},{10,8},{12,... | collective-permute-start | bytes 3145736 | tf_op jit(solution)/shard_map/ppermute | solution.py:466
  1077.4 48.5 %collective-permute-start.33 = (bf16[512,1024]{1,0:T(8,128)(2,1)}, bf16[512,1024]{1,0:T(8,128)(2,1)}, u32[]{:S(2)}, u32[]{:S(2)}) collective-permute-start(bf16[512,1024]{1,0:T(8,128)(2,1)} %get-tuple-element.127), channel_id=1, source_target_pairs={{0,2},{2,4},{4,6},{6,0},{1,3},{3,5},{5,7},{7,1},{8,10},{10,12},{12... | collective-permute-start | bytes 3145736 | tf_op jit(solution)/shard_map/ppermute | solution.py:463
  1081.2 64.0 %collective-permute-start.35 = (bf16[512,1024]{1,0:T(8,128)(2,1)S(1)}, bf16[512,1024]{1,0:T(8,128)(2,1)}, u32[]{:S(2)}, u32[]{:S(2)}) collective-permute-start(bf16[512,1024]{1,0:T(8,128)(2,1)S(1)} %add.153), channel_id=1, source_target_pairs={{0,6},{2,0},{4,2},{6,4},{1,7},{3,1},{5,3},{7,5},{8,14},{10,8},{12,... | collective-permute-start | bytes 3145736 | tf_op jit(solution)/shard_map/ppermute | solution.py:466
  1100.2 77.3 %collective-permute-start.31 = (bf16[512,1024]{1,0:T(8,128)(2,1)}, bf16[512,1024]{1,0:T(8,128)(2,1)}, u32[]{:S(2)}, u32[]{:S(2)}) collective-permute-start(bf16[512,1024]{1,0:T(8,128)(2,1)} %add.152), channel_id=1, source_target_pairs={{0,2},{2,4},{4,6},{6,0},{1,3},{3,5},{5,7},{7,1},{8,10},{10,12},{12... | collective-permute-start | bytes 3145736 | tf_op jit(solution)/shard_map/ppermute | solution.py:463
  1104.8 81.7 %collective-permute-start.62 = (bf16[512,1024]{1,0:T(8,128)(2,1)}, bf16[512,1024]{1,0:T(8,128)(2,1)}, u32[]{:S(2)}, u32[]{:S(2)}) collective-permute-start(bf16[512,1024]{1,0:T(8,128)(2,1)} %get-tuple-element.162), channel_id=1, source_target_pairs={{0,6},{2,0},{4,2},{6,4},{1,7},{3,1},{5,3},{7,5},{8,14},{10,8},{12,... | collective-permute-start | bytes 3145736 | tf_op jit(solution)/shard_map/ppermute | solution.py:466
  1122.7 63.9 %collective-permute-start.63 = (bf16[512,1024]{1,0:T(8,128)(2,1)}, bf16[512,1024]{1,0:T(8,128)(2,1)}, u32[]{:S(2)}, u32[]{:S(2)}) collective-permute-start(bf16[512,1024]{1,0:T(8,128)(2,1)} %get-tuple-element.164), channel_id=1, source_target_pairs={{0,2},{2,4},{4,6},{6,0},{1,3},{3,5},{5,7},{7,1},{8,10},{10,12},{12... | collective-permute-start | bytes 3145736 | tf_op jit(solution)/shard_map/ppermute | solution.py:463
  1125.9 60.7 %collective-permute-start.65 = (bf16[512,1024]{1,0:T(8,128)(2,1)}, bf16[512,1024]{1,0:T(8,128)(2,1)}, u32[]{:S(2)}, u32[]{:S(2)}) collective-permute-start(bf16[512,1024]{1,0:T(8,128)(2,1)} %add.161), channel_id=1, source_target_pairs={{0,6},{2,0},{4,2},{6,4},{1,7},{3,1},{5,3},{7,5},{8,14},{10,8},{12,... | collective-permute-start | bytes 3145736 | tf_op jit(solution)/shard_map/ppermute | solution.py:466
  1183.5 53.8 %collective-permute-start.36 = (bf16[512,1024]{1,0:T(8,128)(2,1)}, bf16[512,1024]{1,0:T(8,128)(2,1)}, u32[]{:S(2)}, u32[]{:S(2)}) collective-permute-start(bf16[512,1024]{1,0:T(8,128)(2,1)} %get-tuple-element.130), channel_id=1, source_target_pairs={{0,24},{8,0},{16,8},{24,16},{1,25},{9,1},{17,9},{25,17},{2,26},{10... | collective-permute-start | bytes 3145736 | tf_op jit(solution)/shard_map/ppermute | solution.py:466
  1192.7 65.9 %collective-permute-start.68 = (bf16[512,1024]{1,0:T(8,128)(2,1)}, bf16[512,1024]{1,0:T(8,128)(2,1)S(1)}, u32[]{:S(2)}, u32[]{:S(2)}) collective-permute-start(bf16[512,1024]{1,0:T(8,128)(2,1)} %get-tuple-element.167), channel_id=1, source_target_pairs={{0,8},{8,16},{16,24},{24,0},{1,9},{9,17},{17,25},{25,1},{2,10},{10... | collective-permute-start | bytes 3145736 | tf_op jit(solution)/shard_map/ppermute | solution.py:463
  1256.4 47.9 %collective-permute-start.71 = (bf16[512,1024]{1,0:T(8,128)(2,1)S(1)}, bf16[512,1024]{1,0:T(8,128)(2,1)S(1)}, u32[]{:S(2)}, u32[]{:S(2)}) collective-permute-start(bf16[512,1024]{1,0:T(8,128)(2,1)S(1)} %copy-done.13), channel_id=1, source_target_pairs={{0,8},{8,16},{16,24},{24,0},{1,9},{9,17},{17,25},{25,1},{2,10},{10... | collective-permute-start | bytes 3145736 | tf_op jit(solution)/shard_map/ppermute | solution.py:463
  (64 other events, 1889.1 us)
Sparse Core Ops, SparseCore 0:
  11.6 39.9 all-gather.6
  53.6 85.6 all-gather.8
  141.0 82.2 all-gather.10
  224.7 47.2 all-gather.12
  273.5 154.2 all-gather.14
  429.3 152.5 all-gather.16
